TPU v7x, 8 devices: a whole 2x2x1 slice. The times are simulated.
8 devices in a mesh: rep: 1 (over z), emb: 2 (over y), model: 4 (over x, core).
Axes of the slice: x: 2, y: 2, z: 1, core: 2. Of those that a mesh axis runs over, the one named last changes fastest.
Arguments:
- x: bfloat16 [512, 8192], P('rep')
- Wq: bfloat16 [8192, 8192], P('emb', 'model')
- Wk: bfloat16 [8192, 256], replicated
- Wv: bfloat16 [8192, 256], replicated
- Wo: bfloat16 [8192, 8192], P('model', 'emb')
- Kc: bfloat16 [512, 2048, 256], P('rep')
- Vc: bfloat16 [512, 2048, 256], P('rep')
- lengths: int32 [512], P('rep')
Outputs:
- output 1: bfloat16 [512, 8192], P('rep')
- output 2: bfloat16 [512, 256], P('rep')
- output 3: bfloat16 [512, 256], P('rep')
All inputs are finite; a program needn't handle non-finite values.
Results may differ from a plain program's by a relative error of at most 0.0108907.
Values are sent between devices in bfloat16 or wider.
A program may use at most 4.25 GiB of HBM per device.

v0:
```python
import jax
import jax.numpy as jnp
from jax import lax
from jax.sharding import PartitionSpec as P


def _attend(q, K, V, kn, vn, lens):
    dh = q.shape[-1]
    t = K.shape[1]
    scale = dh ** -0.5
    s = jnp.einsum('bhd,btd->bht', q, K, preferred_element_type=jnp.float32) * scale
    valid = jnp.arange(t)[None, :] < lens[:, None]
    s = jnp.where(valid[:, None, :], s, -jnp.inf)
    sn = jnp.einsum('bhd,bd->bh', q, kn, preferred_element_type=jnp.float32) * scale
    m = jnp.maximum(jnp.max(s, axis=-1), sn)
    p = jnp.exp(s - m[..., None])
    pn = jnp.exp(sn - m)
    l = jnp.sum(p, axis=-1) + pn
    acc = jnp.einsum('bht,btd->bhd', p.astype(jnp.bfloat16), V, preferred_element_type=jnp.float32)
    acc = acc + pn.astype(jnp.bfloat16).astype(jnp.float32)[..., None] * vn.astype(jnp.float32)[:, None, :]
    return (acc / l[..., None]).astype(jnp.bfloat16)


def solution(mesh):
    ne = mesh.shape['emb']
    nm = mesh.shape['model']

    def local(x, Wq, Wk, Wv, Wo, Kc, Vc, lengths):
        b, d = x.shape
        de = Wq.shape[0]
        dh = Wk.shape[1]
        hl = Wq.shape[1] // dh
        be = b // ne
        bl = be // nm
        i = lax.axis_index('emb')
        j = lax.axis_index('model')
        xi = lax.dynamic_slice_in_dim(x, i * de, de, axis=1)
        qp = jnp.dot(xi, Wq, preferred_element_type=jnp.float32)
        q = lax.psum_scatter(qp, 'emb', scatter_dimension=0, tiled=True)
        q = q.astype(jnp.bfloat16).reshape(be, hl, dh)
        q = lax.all_to_all(q, 'model', 0, 1, tiled=True)
        k_new = jnp.dot(x, Wk, preferred_element_type=jnp.float32).astype(jnp.bfloat16)
        v_new = jnp.dot(x, Wv, preferred_element_type=jnp.float32).astype(jnp.bfloat16)
        start = i * be + j * bl
        K = lax.dynamic_slice_in_dim(Kc, start, bl, 0)
        V = lax.dynamic_slice_in_dim(Vc, start, bl, 0)
        kn = lax.dynamic_slice_in_dim(k_new, start, bl, 0)
        vn = lax.dynamic_slice_in_dim(v_new, start, bl, 0)
        lens = lax.dynamic_slice_in_dim(lengths, start, bl, 0)
        o = _attend(q, K, V, kn, vn, lens)
        o = lax.all_to_all(o, 'model', 1, 0, tiled=True)
        o = lax.all_gather(o, 'emb', axis=0, tiled=True)
        yp = jnp.dot(o.reshape(b, hl * dh), Wo, preferred_element_type=jnp.float32).astype(jnp.bfloat16)
        ys = lax.psum(yp, 'model')
        yi = (xi.astype(jnp.float32) + ys.astype(jnp.float32)).astype(jnp.bfloat16)
        y = lax.all_gather(yi, 'emb', axis=1, tiled=True)
        return y, k_new, v_new

    in_specs = (P('rep', None), P('emb', 'model'), P(), P(), P('model', 'emb'),
                P('rep', None, None), P('rep', None, None), P('rep'))
    out_specs = (P('rep', None), P('rep', None), P('rep', None))
    return jax.shard_map(local, mesh=mesh, in_specs=in_specs, out_specs=out_specs, check_vma=False)
```

profile of v0, /device:TPU:0, one launch (start us, length us, event | category | flops | bytes accessed | tf_op | source)
XLA Modules:
  0.0 436.1 jit_solution(18364988623586563229)
XLA Ops:
  7.2 0.0 reduce-scatter.2.cloned.1.call-start
  7.2 14.9 %fusion.12 = f32[512,2048]{1,0:T(8,128)} fusion(bf16[4096,2048]{1,0:T(8,128)(2,1)} %param.9, bf16[512,8192]{1,0:T(8,128)(2,1)} %param.8, s32[]{:T(128)S(6)} %select_n.14), kind=kOutput, calls=%fused_computation.15 | convolution fusion | flops 8589934592 | bytes 25165828 | tf_op jit(solution)/shard_map/dot_general | solution.py:38
  22.1 0.0 reduce-scatter.2.cloned.1.call-update
  22.1 6.9 %convolution_convert_fusion.2 = bf16[512,256]{1,0:T(8,128)(2,1)S(1)} fusion(bf16[512,8192]{1,0:T(8,128)(2,1)} %param.8, bf16[8192,256]{1,0:T(8,128)(2,1)} %param.10), kind=kOutput, calls=%fused_computation.19 | convolution fusion | flops 2147614720 | bytes 12845056 | tf_op jit(solution)/shard_map/dot_general | solution.py:42
  29.1 0.0 copy-start.1
  29.1 47.6 %reduce-scatter.2.cloned.1.call-done = f32[256,2048]{1,0:T(8,128)} async-done(((f32[512,2048]{1,0:T(8,128)}), f32[256,2048]{1,0:T(8,128)}) %reduce-scatter.2.cloned.1.call-update) | async-done | bytes 2097168 | tf_op jit(solution)/shard_map/reduce_scatter | solution.py:39
  76.6 1.7 convert_element_type.37
  78.4 1.3 copy.23
  79.6 3.5 all-to-all-start
  83.2 0.2 all-gather.3.cloned.1.call-start
  83.4 6.9 %convolution_convert_fusion.1 = bf16[512,256]{1,0:T(8,128)(2,1)S(1)} fusion(bf16[512,8192]{1,0:T(8,128)(2,1)} %param.8, bf16[8192,256]{1,0:T(8,128)(2,1)} %param.11), kind=kOutput, calls=%fused_computation.18 | convolution fusion | flops 2147614720 | bytes 12845056 | tf_op jit(solution)/shard_map/dot_general | solution.py:43
  90.3 0.0 copy-start
  90.3 0.8 dynamic_slice.19
  91.1 0.0 copy-done.1
  91.1 0.1 iota_compare_fusion
  91.3 6.1 %all-to-all-done = bf16[256,8,256]{2,1,0:T(8,128)(2,1)S(1)} async-done(((bf16[256,8,256]{2,1,0:T(8,128)(2,1)}), bf16[256,8,256]{2,1,0:T(8,128)(2,1)S(1)}, u32[]{:S(2)}, u32[]{:S(2)}) %all-to-all-start) | async-done | bytes 1048608 | tf_op jit(solution)/shard_map/all_to_all | solution.py:41
  97.4 0.4 fusion.18
  97.7 33.8 %fusion.4 = (f32[64,32]{1,0:T(8,128)S(1)}, f32[64,32,2048]{2,1,0:T(8,128)}) fusion(pred[64,2048]{1,0:T(8,128)(4,1)S(1)} %iota_compare_fusion, bf16[512,2048,256]{2,1,0:T(8,128)(2,1)} %param.13, s32[]{:T(128)S(6)} %select_n.15, bf16[4,64,8,256]{3,2,1,0:T(8,128)(2,1)S(1)} %bitcast.30), kind=kOutput, calls=%fused_computation.6 | convolution fusion | flops 2160064512 | bytes 85073920 | tf_op jit(solution)/shard_map/bhd,btd->bht/dot_general | solution.py:11
  131.6 0.0 copy-done
  131.6 8.1 %fusion.5 = f32[64,32]{1,0:T(8,128)S(1)} fusion(f32[64,32,2048]{2,1,0:T(8,128)} %get-tuple-element.6, f32[64,32]{1,0:T(8,128)S(1)} %multiply_maximum_fusion, pred[64,2048]{1,0:T(8,128)(4,1)S(1)} %iota_compare_fusion), kind=kLoop, calls=%fused_computation.7 | loop fusion | flops 16775168 | bytes 16924672 | tf_op jit(solution)/shard_map/reduce_sum | solution.py:18
  139.7 28.0 %divide_convert_fusion = bf16[64,32,256]{2,1,0:T(8,128)(2,1)S(1)} fusion(bf16[512,2048,256]{2,1,0:T(8,128)(2,1)} %param.14, s32[]{:T(128)S(6)} %select_n.15, f32[64,32,2048]{2,1,0:T(8,128)} %get-tuple-element.6, f32[64,32]{1,0:T(8,128)S(1)} %multiply_maximum_fusion, pred[64,2048]{1,0:T(8,128)(4,1)S(1)} %iota_compare_fusion, ...), kind=kOutput, calls=%fused_computation.17 | convolution fusion | flops 2166358016 | bytes 85155840 | tf_op jit(solution)/shard_map/bht,btd->bhd/dot_general | solution.py:19
  167.7 0.6 copy.17
  168.3 16.9 %all_to_all.36 = bf16[64,32,256]{2,0,1:T(8,128)(2,1)S(1)} all-to-all(bf16[64,32,256]{2,0,1:T(8,128)(2,1)S(1)} %copy.17), channel_id=1, replica_groups=mesh['rep'=1,'emb'=2,'model'=4] {'model'}, dimensions={1} | all-to-all | bytes 2097152 | tf_op jit(solution)/shard_map/all_to_all | solution.py:51
  185.2 1.6 copy.19
  186.7 0.0 all-gather.3.cloned.1.call-update
  186.8 0.3 all-reduce.2.cloned.1.call-start
  187.0 28.9 %all-gather.3.cloned.1.call-done = bf16[512,8,256]{2,1,0:T(8,128)(2,1)} async-done(((bf16[256,8,256]{2,1,0:T(8,128)(2,1)}), bf16[512,8,256]{2,1,0:T(8,128)(2,1)}) %all-gather.3.cloned.1.call-update) | async-done | bytes 2097168 | tf_op jit(solution)/shard_map/all_gather | solution.py:52
  216.0 2.3 copy.24
  218.2 13.7 %convolution_convert_fusion = bf16[512,4096]{1,0:T(8,128)(2,1)} fusion(bf16[512,2048]{1,0:T(8,128)(2,1)S(1)} %bitcast.35, bf16[2048,4096]{1,0:T(8,128)(2,1)} %param.12), kind=kOutput, calls=%fused_computation.14 | convolution fusion | flops 8592031744 | bytes 23068672 | tf_op jit(solution)/shard_map/dot_general | solution.py:53
  232.0 0.0 all-reduce.2.cloned.1.call-update
  232.0 0.0 all-gather.5.cloned.1.call-start
  232.0 79.9 %all-reduce.2.cloned.1.call-done = bf16[512,4096]{1,0:T(8,128)(2,1)} async-done(((bf16[512,4096]{1,0:T(8,128)(2,1)}), bf16[512,4096]{1,0:T(8,128)(2,1)}) %all-reduce.2.cloned.1.call-update) | async-done | bytes 4194320 | tf_op jit(solution)/shard_map/psum | solution.py:54
  311.9 7.2 %add_convert_fusion = bf16[512,4096]{1,0:T(8,128)(2,1)} fusion(bf16[512,4096]{1,0:T(8,128)(2,1)} %all-reduce.2.cloned.1.call-done, bf16[512,8192]{1,0:T(8,128)(2,1)} %param.8, s32[]{:T(128)S(6)} %select_n.14), kind=kLoop, calls=%fused_computation.9 | loop fusion | flops 8388608 | bytes 12582916 | tf_op jit(solution)/shard_map/convert_element_type | solution.py:55
  319.1 0.0 all-gather.5.cloned.1.call-update
  319.2 102.6 %all-gather.5.cloned.1.call-done = bf16[512,8192]{1,0:T(8,128)(2,1)} async-done(((bf16[512,4096]{1,0:T(8,128)(2,1)}), bf16[512,8192]{1,0:T(8,128)(2,1)}) %all-gather.5.cloned.1.call-update) | async-done | bytes 8388624 | tf_op jit(solution)/shard_map/all_gather | solution.py:56
  421.7 7.8 %copy.39 = bf16[512,8192]{1,0:T(8,128)(2,1)} copy(bf16[512,8192]{1,0:T(8,128)(2,1)} %all-gather.5.cloned.1.call-done) | data formatting | bytes 16777216
  (4 shorter events, 0.0 us)
Async XLA Ops:
  7.2 69.5 %reduce-scatter.2.cloned.1.call-start = ((), (), s32[]{:S(2)}) async-start(), calls=%async_computation.3 | async-start | bytes 6291456 | tf_op jit(solution)/shard_map/reduce_scatter | solution.py:39
  29.1 62.1 %copy-start.1 = (bf16[512,256]{1,0:T(8,128)(2,1)}, bf16[512,256]{1,0:T(8,128)(2,1)S(1)}, u32[]{:S(2)}) copy-start(bf16[512,256]{1,0:T(8,128)(2,1)S(1)} %convolution_convert_fusion.2) | copy-start | bytes 786436
  79.6 17.7 %all-to-all-start = ((bf16[256,8,256]{2,1,0:T(8,128)(2,1)}), bf16[256,8,256]{2,1,0:T(8,128)(2,1)S(1)}, u32[]{:S(2)}, u32[]{:S(2)}) async-start(bf16[256,8,256]{2,1,0:T(8,128)(2,1)} %bitcast.12), calls=%async_computation.1 | async-start | bytes 2097152 | tf_op jit(solution)/shard_map/all_to_all | solution.py:41
  83.2 132.8 %all-gather.3.cloned.1.call-start = ((), (), s32[]{:S(2)}) async-start(), calls=%async_computation.4 | async-start | bytes 3145728 | tf_op jit(solution)/shard_map/all_gather | solution.py:52
  90.3 41.3 %copy-start = (bf16[512,256]{1,0:T(8,128)(2,1)}, bf16[512,256]{1,0:T(8,128)(2,1)S(1)}, u32[]{:S(2)}) copy-start(bf16[512,256]{1,0:T(8,128)(2,1)S(1)} %convolution_convert_fusion.1) | copy-start | bytes 786436
  186.8 125.1 %all-reduce.2.cloned.1.call-start = ((), (), s32[]{:S(2)}) async-start(), calls=%async_computation.5 | async-start | bytes 8388608 | tf_op jit(solution)/shard_map/psum | solution.py:54
  232.0 189.8 %all-gather.5.cloned.1.call-start = ((), (), s32[]{:S(2)}) async-start(), calls=%async_computation.6 | async-start | bytes 12582912 | tf_op jit(solution)/shard_map/all_gather | solution.py:56
Sparse Core Ops, SparseCore 0:
  22.3 54.3 reduce-scatter.1
  186.9 29.0 all-gather.2
  232.1 79.7 all-reduce.1
  319.3 102.4 all-gather.4
where the time goes:
time: 437 us; the launch traced here: 436 us
  waiting for transfers between devices  265 us (61%)
  matrix products  105 us (24%)
  other arithmetic  17.2 us (4%)
  blocking collectives  16.9 us (4%)
  local copies, waits for them, and re-layouts  14.3 us (3%)
  between operations  13.9 us (3%)
    all_gather x1, waiting for transfers between devices, local(): y = lax.all_gather(yi, 'emb', axis=1, tiled=True)  103 us
    psum x1, waiting for transfers between devices, local(): ys = lax.psum(yp, 'model')  79.9 us
    reduce_scatter x1, waiting for transfers between devices, local(): q = lax.psum_scatter(qp, 'emb', scatter_dimension=0, tiled=True)  47.6 us
    dot_general x1, matrix products, _attend(): jnp.einsum('bhd,btd->bht', q, K, preferred_element_type=jnp.float32) * scale  33.8 us
    all_gather x1, waiting for transfers between devices, local(): o = lax.all_gather(o, 'emb', axis=0, tiled=True)  28.9 us
    dot_general x1, matrix products, _attend(): jnp.einsum('bht,btd->bhd', p.astype(jnp.bfloat16), V, preferred_element_t...  28 us
    all_to_all x1, blocking collectives, local(): o = lax.all_to_all(o, 'model', 1, 0, tiled=True)  16.9 us
    dot_general x1, matrix products, local(): qp = jnp.dot(xi, Wq, preferred_element_type=jnp.float32)  14.9 us
  transfers between devices with their start and end apart: 5, of which 5 were waited for; matrix products, arithmetic and copies ran while one was open for 3% of the time, Pallas kernels for 0%

commit v1 on v0

v1 whole, which is shorter than its diff:
```python
import functools

import jax
import jax.numpy as jnp
from jax import lax
from jax.experimental import pallas as pl
from jax.experimental.pallas import tpu as pltpu
from jax.sharding import PartitionSpec as P

MESH = pl.DeviceIdType.MESH
BK = 512
G = 4
RING = 6
AHEAD = 4
CH = 4
SUB = 2
NH = 8


def _vmem():
    return pl.BlockSpec(memory_space=pltpu.VMEM)


def _any():
    return pl.BlockSpec(memory_space=pl.ANY)


def _smem():
    return pl.BlockSpec(memory_space=pltpu.SMEM)


def _attn_kernel(scale, seqs, blks, lens, meta, q_ref, kn_ref, vn_ref, kc, vc, o_ref,
                 kbuf, vbuf, pbuf, mbuf, lbuf, mrun, lrun, arun, ksem, vsem):
    start = meta[0]
    steps = meta[1]

    def copies(g):
        slot = lax.rem(g, RING)
        out = []
        for u in range(G):
            n = g * G + u
            row = start + seqs[n] % q_ref.shape[0]
            span = pl.ds(pl.multiple_of(blks[n] * BK, BK), BK)
            out.append((pltpu.make_async_copy(kc.at[row, span], kbuf.at[slot, u], ksem.at[slot, u]),
                        pltpu.make_async_copy(vc.at[row, span], vbuf.at[slot, u], vsem.at[slot, u])))
        return out

    def fetch(g):
        for ck, cv in copies(g):
            ck.start()
            cv.start()

    def insert(buf, slot, u, row, new):
        base = pl.multiple_of(jnp.clip(row // 16, 0, BK // 16 - 1) * 16, 16)
        old = buf[slot, u, pl.ds(base, 16), :]
        at = lax.broadcasted_iota(jnp.int32, (16, 1), 0) + base == row
        buf[slot, u, pl.ds(base, 16), :] = jnp.where(at, new, old.astype(jnp.float32)).astype(jnp.bfloat16)

    def scores(g):
        slot = lax.rem(g, RING)
        half = lax.rem(g, 2)
        for ck, _ in copies(g):
            ck.wait()
        for u in range(G):
            n = g * G + u
            seq = seqs[n]
            sq = seq % q_ref.shape[0]
            row = lens[seq] - blks[n] * BK
            insert(kbuf, slot, u, row, kn_ref[sq].astype(jnp.float32))
            s = lax.dot_general(q_ref[sq], kbuf[slot, u], (((1,), (1,)), ((), ())),
                                preferred_element_type=jnp.float32) * scale
            s = jnp.where(lax.broadcasted_iota(jnp.int32, s.shape, 1) <= row, s, -jnp.inf)
            m = jnp.max(s, axis=1, keepdims=True)
            p = jnp.exp(s - m)
            pbuf[half, u] = p.astype(jnp.bfloat16)
            mbuf[half, u] = jnp.broadcast_to(m, mbuf.shape[2:])
            lbuf[half, u] = jnp.broadcast_to(jnp.sum(p, axis=1, keepdims=True), lbuf.shape[2:])

    def values(g):
        slot = lax.rem(g, RING)
        half = lax.rem(g, 2)
        for _, cv in copies(g):
            cv.wait()
        accs = []
        for u in range(G):
            n = g * G + u
            seq = seqs[n]
            row = lens[seq] - blks[n] * BK
            insert(vbuf, slot, u, row, vn_ref[seq % q_ref.shape[0]].astype(jnp.float32))
            accs.append(jnp.dot(pbuf[half, u], vbuf[slot, u], preferred_element_type=jnp.float32))
        mo, lo, ao = mrun[...], lrun[...], arun[...]
        for u in range(G):
            n = g * G + u
            first = blks[n] == 0
            mo = jnp.where(first, -1e30, mo)
            lo = jnp.where(first, 0.0, lo)
            ao = jnp.where(first, 0.0, ao)
            m = jnp.maximum(mo, mbuf[half, u])
            alpha = jnp.exp(mo - m)
            beta = jnp.exp(mbuf[half, u] - m)
            lo = lo * alpha + lbuf[half, u] * beta
            ao = ao * jnp.concatenate([alpha, alpha], 1) + accs[u] * jnp.concatenate([beta, beta], 1)
            mo = m
            inv = 1.0 / lo
            o_ref[seqs[n]] = (ao * jnp.concatenate([inv, inv], 1)).astype(jnp.bfloat16)
        mrun[...] = mo
        lrun[...] = lo
        arun[...] = ao

    mrun[...] = jnp.zeros_like(mrun)
    lrun[...] = jnp.zeros_like(lrun)
    arun[...] = jnp.zeros_like(arun)
    for g in range(AHEAD):
        @pl.when(g < steps)
        def _():
            fetch(g)

    @pl.when(AHEAD < steps)
    def _():
        fetch(AHEAD)

    scores(0)

    def body(g, c):
        @pl.when(g + AHEAD < steps)
        def _():
            fetch(g + AHEAD)

        values(g - 1)
        scores(g)
        return c

    lax.fori_loop(1, steps, body, 0)
    values(steps - 1)


def _attend(q, kn, vn, Kc, Vc, lens, start):
    nb, h, dh = q.shape
    t = Kc.shape[1]
    assert dh == 256 and t % BK == 0
    blocks = lens // BK + 1
    cum = jnp.sum(jnp.where(jnp.arange(nb)[None, :] <= jnp.arange(nb)[:, None], blocks[None, :], 0), axis=1)
    most = nb * (t // BK) + G
    n = jnp.arange(most)
    seqs = jnp.sum((cum[None, :] <= n[:, None]).astype(jnp.int32), axis=1)
    before = jnp.max(jnp.where(cum[None, :] <= n[:, None], cum[None, :], 0), axis=1)
    blks = jnp.where(seqs < nb, n - before, 0)
    steps = (cum[-1] + G - 1) // G
    meta = jnp.stack([start, steps]).astype(jnp.int32)
    lens1 = jnp.concatenate([lens, jnp.ones((8,), jnp.int32)])
    bf, f32 = jnp.bfloat16, jnp.float32
    out = pl.pallas_call(
        functools.partial(_attn_kernel, dh ** -0.5),
        out_shape=jax.ShapeDtypeStruct((nb + 1, h, dh), bf),
        in_specs=[_smem()] * 4 + [_vmem()] * 3 + [_any()] * 2,
        out_specs=_vmem(),
        scratch_shapes=[
            pltpu.VMEM((RING, G, BK, dh), bf), pltpu.VMEM((RING, G, BK, dh), bf),
            pltpu.VMEM((2, G, h, BK), bf), pltpu.VMEM((2, G, h, 128), f32), pltpu.VMEM((2, G, h, 128), f32),
            pltpu.VMEM((h, 128), f32), pltpu.VMEM((h, 128), f32), pltpu.VMEM((h, dh), f32),
            pltpu.SemaphoreType.DMA((RING, G)), pltpu.SemaphoreType.DMA((RING, G)),
        ],
        name="attend",
    )(seqs.astype(jnp.int32), blks.astype(jnp.int32), lens1, meta, q, kn.reshape(nb, 1, dh), vn.reshape(nb, 1, dh), Kc, Vc)
    return out[:nb]


def _out_kernel(ne, nm, o_ref, wo, x, y, wv, xv, ob, pown, psend, precv, ssend, srecv, ybuf, yrecv,
                wsem, xsem, lsem, osend, orecv, psend_s, precv_s, ssend_s, srecv_s,
                cs, cr, es, er, fs, fr):
    i = lax.axis_index("emb")
    j = lax.axis_index("model")
    me = i * nm + j
    c = lax.rem(j, 2)
    jp = j + 1 - 2 * c
    jx = lax.rem(j + 2, nm)
    ie = 1 - i
    half = wv.shape[2]
    cw = half // SUB
    rows = o_ref.shape[0] // CH
    kk = wv.shape[1]
    dev = ne * nm

    def at(a, b):
        return {"emb": a, "model": b}

    barrier = pltpu.get_barrier_semaphore()
    for r in range(1, dev):
        d = lax.rem(me + r, dev)
        pl.semaphore_signal(barrier, inc=1, device_id=at(d // nm, lax.rem(d, nm)), device_id_type=MESH)
    pl.semaphore_wait(barrier, dev - 1)

    def osend_copy(s, r):
        d = lax.rem(me + r, dev)
        dj = lax.rem(d, nm)
        return pltpu.make_async_remote_copy(
            src_ref=o_ref.at[pl.ds(pl.multiple_of(s * rows, rows), rows), pl.ds(pl.multiple_of(dj * kk, kk), kk)],
            dst_ref=ob.at[s, pl.ds(pl.multiple_of(me * rows, rows), rows), :],
            send_sem=osend.at[s, r], recv_sem=orecv.at[s, dev - r],
            device_id=at(d // nm, dj), device_id_type=MESH)

    def orecv_copy(s, r):
        d = lax.rem(me + r, dev)
        return pltpu.make_async_remote_copy(
            src_ref=ob.at[s, pl.ds(pl.multiple_of(d * rows, rows), rows), :],
            dst_ref=ob.at[s, pl.ds(pl.multiple_of(d * rows, rows), rows), :],
            send_sem=osend.at[s, r], recv_sem=orecv.at[s, r],
            device_id=at(d // nm, lax.rem(d, nm)), device_id_type=MESH)

    for s in range(CH):
        for r in (4, 6, 5, 7, 2, 3, 1):
            osend_copy(s, r).start()

    def wcopy(b, u):
        col = pl.multiple_of((1 - c if b == 0 else c) * half + u * cw, cw)
        return pltpu.make_async_copy(wo.at[:, pl.ds(col, cw)], wv.at[b, :, pl.ds(u * cw, cw)], wsem.at[b, u])

    for b in range(2):
        for u in range(SUB):
            wcopy(b, u).start()
    mycol = pl.multiple_of((i * 2 + c) * half, half)
    excol = pl.multiple_of(((1 - i) * 2 + c) * half, half)
    xcopy = pltpu.make_async_copy(x.at[:, :, pl.ds(mycol, half)], xv, xsem)
    xcopy.start()
    for s in range(CH):
        ob[s, pl.ds(pl.multiple_of(me * rows, rows), rows), :] = o_ref[
            pl.ds(s * rows, rows), pl.ds(pl.multiple_of(j * kk, kk), kk)]
    for b in range(2):
        for u in range(SUB):
            wcopy(b, u).wait()
    xcopy.wait()

    def pcopy(s, u):
        return pltpu.make_async_remote_copy(
            src_ref=psend.at[s, u], dst_ref=precv.at[s, u], send_sem=psend_s.at[s, u], recv_sem=precv_s.at[s, u],
            device_id=at(i, jp), device_id_type=MESH)

    def scopy(s, u):
        return pltpu.make_async_remote_copy(
            src_ref=ssend.at[s, u], dst_ref=srecv.at[s, u], send_sem=ssend_s.at[s, u], recv_sem=srecv_s.at[s, u],
            device_id=at(i, jx), device_id_type=MESH)

    def yref(s, u, base):
        return y.at[:, pl.ds(pl.multiple_of(s * rows, rows), rows), pl.ds(pl.multiple_of(base + u * cw, cw), cw)]

    def ccopy(s, u):
        return pltpu.make_async_remote_copy(
            src_ref=ybuf.at[s, u], dst_ref=yref(s, u, mycol), send_sem=cs.at[s, u], recv_sem=cr.at[s, u],
            device_id=at(i, jp), device_id_type=MESH)

    def ecopy(s, u):
        return pltpu.make_async_remote_copy(
            src_ref=ybuf.at[s, u], dst_ref=yrecv.at[s, u], send_sem=es.at[s, u], recv_sem=er.at[s, u],
            device_id=at(ie, j), device_id_type=MESH)

    def fcopy(s, u):
        return pltpu.make_async_remote_copy(
            src_ref=yrecv.at[s, u], dst_ref=yref(s, u, excol), send_sem=fs.at[s, u], recv_sem=fr.at[s, u],
            device_id=at(i, jp), device_id_type=MESH)

    def lcopy(s, u, k):
        if k == 0:
            return pltpu.make_async_copy(ybuf.at[s, u], yref(s, u, mycol), lsem.at[0, s, u])
        return pltpu.make_async_copy(yrecv.at[s, u], yref(s, u, excol), lsem.at[1, s, u])

    def compute(s):
        for r in range(1, dev):
            orecv_copy(s, r).wait_recv()
        lhs = ob[s]
        for u in range(SUB):
            psend[s, u] = jnp.dot(lhs, wv[0, :, u * cw:(u + 1) * cw],
                                  preferred_element_type=jnp.float32).astype(jnp.bfloat16)
            pcopy(s, u).start()
        for u in range(SUB):
            pown[u] = jnp.dot(lhs, wv[1, :, u * cw:(u + 1) * cw], preferred_element_type=jnp.float32)
        for u in range(SUB):
            pcopy(s, u).wait_recv()
            ssend[s, u] = (pown[u] + precv[s, u].astype(jnp.float32)).astype(jnp.bfloat16)
            scopy(s, u).start()

    def finish(s):
        for u in range(SUB):
            scopy(s, u).wait_recv()
            tot = ssend[s, u].astype(jnp.float32) + srecv[s, u].astype(jnp.float32)
            xs = xv[:, pl.ds(pl.multiple_of(s * rows, rows), rows), u * cw:(u + 1) * cw].astype(jnp.float32)
            ybuf[s, u] = (xs + tot.reshape(dev, rows, cw)).astype(jnp.bfloat16)
            ecopy(s, u).start()
            ccopy(s, u).start()
            lcopy(s, u, 0).start()

    def forward(s):
        for u in range(SUB):
            ecopy(s, u).wait_recv()
            fcopy(s, u).start()
            lcopy(s, u, 1).start()

    def step(s, carry):
        compute(s)

        @pl.when(s >= 1)
        def _():
            finish(s - 1)

        @pl.when(s >= 2)
        def _():
            forward(s - 2)

        return carry

    lax.fori_loop(0, CH, step, 0)
    finish(CH - 1)
    forward(CH - 2)
    forward(CH - 1)
    for s in range(CH):
        for r in range(1, dev):
            osend_copy(s, r).wait_send()
        for u in range(SUB):
            pcopy(s, u).wait_send()
            scopy(s, u).wait_send()
            ecopy(s, u).wait_send()
            ccopy(s, u).wait()
            fcopy(s, u).wait()
            lcopy(s, u, 0).wait()
            lcopy(s, u, 1).wait()


def _project_out(o, Wo, x, ne, nm):
    bl, full = o.shape
    kk, ncol = Wo.shape
    half = ncol // 2
    dev = ne * nm
    rows = bl // CH
    cw = half // SUB
    b, d = x.shape
    bf, f32 = jnp.bfloat16, jnp.float32
    dma = pltpu.SemaphoreType.DMA
    pieces = pltpu.VMEM((CH, SUB, dev * rows, cw), bf)
    pieces3 = pltpu.VMEM((CH, SUB, dev, rows, cw), bf)
    pair = [dma((CH, SUB)), dma((CH, SUB))]
    y = pl.pallas_call(
        functools.partial(_out_kernel, ne, nm),
        out_shape=jax.ShapeDtypeStruct((dev, bl, d), bf),
        in_specs=[_vmem(), _any(), _any()],
        out_specs=_any(),
        scratch_shapes=[
            pltpu.VMEM((2, kk, half), bf), pltpu.VMEM((dev, bl, half), bf), pltpu.VMEM((CH, dev * rows, kk), bf),
            pltpu.VMEM((SUB, dev * rows, cw), f32), pieces, pieces, pieces, pieces, pieces3, pieces3,
            dma((2, SUB)), dma, dma((2, CH, SUB)), dma((CH, dev)), dma((CH, dev)),
        ] + pair * 5,
        compiler_params=pltpu.CompilerParams(collective_id=1, has_side_effects=True, vmem_limit_bytes=60 << 20),
        name="project_out",
    )(o, Wo, x.reshape(dev, bl, d))
    return y.reshape(b, d)


def _in_kernel(ne, nm, x, wq, wk, wv, q, k_out, v_out, xv, wqv, wkv, qsend, qrecv, qown, qb,
               xsem, wsem, ksem, ss, sr, hs, hr, ls):
    i = lax.axis_index("emb")
    j = lax.axis_index("model")
    ie = 1 - i
    de = wq.shape[0]
    be = xv.shape[1] // 2
    bl = be // nm
    cw = wq.shape[1] // NH
    dh = wk.shape[1]

    def at(a, b):
        return {"emb": a, "model": b}

    def xcopy(a, r):
        row = pl.multiple_of((ie if a == 0 else i) * be, be)
        col = pl.multiple_of((i if r == 0 else ie) * de, de)
        return pltpu.make_async_copy(x.at[pl.ds(row, be), pl.ds(col, de)], xv.at[r, a * be:(a + 1) * be, :], xsem.at[a, r])

    def wcopy(h):
        return pltpu.make_async_copy(wq.at[:, pl.ds(h * cw, cw)], wqv.at[h], wsem.at[h])

    def kcopy(n, r):
        src = wk if n == 0 else wv
        row = pl.multiple_of((i if r == 0 else ie) * de, de)
        return pltpu.make_async_copy(src.at[pl.ds(row, de), :], wkv.at[n, r], ksem.at[n, r])

    xcopy(0, 0).start()
    for h in range(NH):
        wcopy(h).start()
    xcopy(1, 0).start()
    xcopy(0, 1).start()
    xcopy(1, 1).start()
    for n in range(2):
        for r in range(2):
            kcopy(n, r).start()

    barrier = pltpu.get_barrier_semaphore()
    pl.semaphore_signal(barrier, inc=1, device_id=at(ie, j), device_id_type=MESH)
    for r in range(1, nm):
        pl.semaphore_signal(barrier, inc=1, device_id=at(i, lax.rem(j + r, nm)), device_id_type=MESH)
    pl.semaphore_wait(barrier, nm)

    def scopy(h):
        return pltpu.make_async_remote_copy(
            src_ref=qsend.at[h], dst_ref=qrecv.at[h], send_sem=ss.at[h], recv_sem=sr.at[h],
            device_id=at(ie, j), device_id_type=MESH)

    def hcopy(h, r):
        d = lax.rem(j + r, nm)
        return pltpu.make_async_remote_copy(
            src_ref=qb.at[h, pl.ds(pl.multiple_of(d * bl, bl), bl), :],
            dst_ref=q.at[:, pl.ds(pl.multiple_of((j * NH + h) * cw, cw), cw)],
            send_sem=hs.at[h, r], recv_sem=hr.at[h, nm - r],
            device_id=at(i, d), device_id_type=MESH)

    def hrecv(h, r):
        d = lax.rem(j + r, nm)
        return pltpu.make_async_remote_copy(
            src_ref=qb.at[h, pl.ds(0, bl), :],
            dst_ref=q.at[:, pl.ds(pl.multiple_of((d * NH + h) * cw, cw), cw)],
            send_sem=hs.at[h, r], recv_sem=hr.at[h, r],
            device_id=at(i, d), device_id_type=MESH)

    def hself(h):
        return pltpu.make_async_copy(
            qb.at[h, pl.ds(pl.multiple_of(j * bl, bl), bl), :],
            q.at[:, pl.ds(pl.multiple_of((j * NH + h) * cw, cw), cw)], ls.at[h])

    xcopy(0, 0).wait()
    for h in range(NH):
        wcopy(h).wait()
        qsend[h] = jnp.dot(xv[0, :be, :], wqv[h], preferred_element_type=jnp.float32)
        scopy(h).start()
    xcopy(1, 0).wait()
    for h in range(NH):
        qown[h] = jnp.dot(xv[0, be:, :], wqv[h], preferred_element_type=jnp.float32)

    xcopy(0, 1).wait()
    xcopy(1, 1).wait()
    for n in range(2):
        for r in range(2):
            kcopy(n, r).wait()
    for n, out in ((0, k_out), (1, v_out)):
        for a in range(2):
            acc = jnp.dot(xv[0, a * be:(a + 1) * be, :], wkv[n, 0], preferred_element_type=jnp.float32)
            acc += jnp.dot(xv[1, a * be:(a + 1) * be, :], wkv[n, 1], preferred_element_type=jnp.float32)
            out[pl.ds(pl.multiple_of((ie if a == 0 else i) * be, be), be), :] = acc.astype(jnp.bfloat16)

    for h in range(NH):
        scopy(h).wait_recv()
        qb[h] = (qown[h] + qrecv[h]).astype(jnp.bfloat16)
        for r in (2, 3, 1):
            hcopy(h, r).start()
        hself(h).start()
    for h in range(NH):
        scopy(h).wait_send()
        hself(h).wait()
        for r in range(1, nm):
            hcopy(h, r).wait_send()
            hrecv(h, r).wait_recv()


def _project_in(x, Wq, Wk, Wv, ne, nm):
    b, d = x.shape
    de, hw = Wq.shape
    dh = Wk.shape[1]
    be = b // ne
    bl = be // nm
    cw = hw // NH
    bf, f32 = jnp.bfloat16, jnp.float32
    dma = pltpu.SemaphoreType.DMA
    return pl.pallas_call(
        functools.partial(_in_kernel, ne, nm),
        out_shape=(jax.ShapeDtypeStruct((bl, hw * nm), bf), jax.ShapeDtypeStruct((b, dh), bf),
                   jax.ShapeDtypeStruct((b, dh), bf)),
        in_specs=[_any()] * 4,
        out_specs=(_any(), _vmem(), _vmem()),
        scratch_shapes=[
            pltpu.VMEM((2, b, de), bf), pltpu.VMEM((NH, de, cw), bf), pltpu.VMEM((2, 2, de, dh), bf),
            pltpu.VMEM((NH, be, cw), f32), pltpu.VMEM((NH, be, cw), f32), pltpu.VMEM((NH, be, cw), f32),
            pltpu.VMEM((NH, be, cw), bf),
            dma((2, 2)), dma((NH,)), dma((2, 2)), dma((NH,)), dma((NH,)), dma((NH, nm)), dma((NH, nm)), dma((NH,)),
        ],
        compiler_params=pltpu.CompilerParams(collective_id=0, has_side_effects=True, vmem_limit_bytes=60 << 20),
        name="project_in",
    )(x, Wq, Wk, Wv)


def solution(mesh):
    ne = mesh.shape['emb']
    nm = mesh.shape['model']

    def local(x, Wq, Wk, Wv, Wo, Kc, Vc, lengths):
        b, d = x.shape
        dh = Wk.shape[1]
        heads = Wq.shape[1] // dh * nm
        be = b // ne
        bl = be // nm
        i = lax.axis_index('emb')
        j = lax.axis_index('model')
        start = i * be + j * bl
        q, k_new, v_new = _project_in(x, Wq, Wk, Wv, ne, nm)
        kn = lax.dynamic_slice_in_dim(k_new, start, bl, 0)
        vn = lax.dynamic_slice_in_dim(v_new, start, bl, 0)
        lens = lax.dynamic_slice_in_dim(lengths, start, bl, 0)
        o = _attend(q.reshape(bl, heads, dh), kn, vn, Kc, Vc, lens, start)
        y = _project_out(o.reshape(bl, heads * dh), Wo, x, ne, nm)
        return y, k_new, v_new

    in_specs = (P('rep', None), P('emb', 'model'), P(), P(), P('model', 'emb'),
                P('rep', None, None), P('rep', None, None), P('rep'))
    out_specs = (P('rep', None), P('rep', None), P('rep', None))
    return jax.shard_map(local, mesh=mesh, in_specs=in_specs, out_specs=out_specs, check_vma=False)
```

time: 437 us -> 207 us (0.47)
  waiting for transfers between devices: 265 us -> 0 us
  Pallas kernels: 0 us -> 186 us
  matrix products: 105 us -> 0 us
  blocking collectives: 16.9 us -> 0 us
  other arithmetic: 17.2 us -> 2.11 us
  between operations: 13.9 us -> 1.38 us
    pallas_call x0 -> x3, Pallas kernels: none -> 186 us  [the longest x1 82.6 us: _project_out(): pl.pallas_call(functools.partial(_out_kernel, ne, nm), out_shape=jax.Shap...]
    all_gather x2 -> x0, waiting for transfers between devices: 132 us -> none  [the longest x1 103 us: local(): y = lax.all_gather(yi, 'emb', axis=1, tiled=True)]
    dot_general x7 -> x0, matrix products: 105 us -> none  [the longest x1 33.8 us: _attend(): jnp.einsum('bhd,btd->bht', q, K, preferred_element_type=jnp.float32) * scale]
    psum x1 -> x0, waiting for transfers between devices: 79.9 us -> none  [local(): ys = lax.psum(yp, 'model')]
    reduce_scatter x1 -> x0, waiting for transfers between devices: 47.6 us -> none  [local(): q = lax.psum_scatter(qp, 'emb', scatter_dimension=0, tiled=True)]
    all_to_all x1 -> x0, blocking collectives: 16.9 us -> none  [local(): o = lax.all_to_all(o, 'model', 1, 0, tiled=True)]
    convert_element_type x4 -> x0, other arithmetic: 9.01 us -> none  [the longest x1 7.25 us: local(): yi = (xi.astype(jnp.float32) + ys.astype(jnp.float32)).astype(jnp.bfloat16)]
    reduce_sum x1, other arithmetic: 8.09 us -> 0.11 us  [_attend(): jnp.sum(jnp.where(jnp.arange(nb)[None, :] <= jnp.arange(nb)[:, None], blo...]
  transfers between devices with their start and end apart: 5 -> 0, of which waited for: 5 -> 0; matrix products, arithmetic and copies ran while one was open for 3% -> 0% of each run, Pallas kernels for 0% -> 0%
where the time goes in v1:
time: 207 us; the launch traced here: 208 us
  Pallas kernels  186 us (90%)
  local copies, waits for them, and re-layouts  17.9 us (9%)
  other arithmetic  2.11 us (1%)
    pallas_call x1, Pallas kernels, _project_out(): pl.pallas_call(functools.partial(_out_kernel, ne, nm), out_shape=jax.Shap...  82.6 us
    pallas_call x1, Pallas kernels, _project_in(): pl.pallas_call(functools.partial(_in_kernel, ne, nm), out_shape=(jax.Shap...  60.1 us
    pallas_call x1, Pallas kernels, _attend(): pl.pallas_call(functools.partial(_attn_kernel, dh ** (-0.5)), out_shape=j...  43.5 us
    unnamed x11, local copies, waits for them, and re-layouts  13.3 us

profile of v1, /device:TPU:0, one launch (start us, length us, event | category | flops | bytes accessed | tf_op | source)
XLA Modules:
  0.0 207.6 jit_solution(4956308637267617294)
XLA Ops:
  0.6 0.8 fusion
  1.4 0.1 select_reduce_fusion.1
  1.5 0.6 slice.6
  2.8 0.6 pad_add_fusion.meta
  3.3 0.5 concatenate.3.lens
  3.9 0.1 select_reduce_fusion
  4.0 0.0 copy-start.2
  4.0 0.6 subtract_select_fusion.blks
  4.6 60.1 %project_in.1 = (bf16[64,8192]{1,0:T(8,128)(2,1)}, bf16[512,256]{1,0:T(8,128)(2,1)}, bf16[512,256]{1,0:T(8,128)(2,1)}) custom-call(bf16[512,8192]{1,0:T(8,128)(2,1)} %x.3, bf16[4096,2048]{1,0:T(8,128)(2,1)} %wq.1, bf16[8192,256]{1,0:T(8,128)(2,1)} %wk.1, bf16[8192,256]{1,0:T(8,128)(2,1)} %wv.1), custom_call_target="tpu_custom_call" | custom-call | tf_op jit(solution)/shard_map/project_in/pallas_call | solution.py:468
  64.7 0.0 copy-done.2
  64.7 2.5 %copy.15 = bf16[8,8,32,256]{3,2,1,0:T(8,128)(2,1)} copy(bf16[8,8,32,256]{3,1,2,0:T(8,128)(2,1)} %bitcast.18) | data formatting | bytes 2097152
  67.2 0.8 dynamic-slice_bitcast_fusion
  68.0 0.7 copy.14.vn_ref
  68.7 0.7 copy.13.kn_ref
  69.3 43.5 %attend.1 = bf16[65,32,256]{2,1,0:T(8,128)(2,1)} custom-call(s32[260]{0:T(512)} %copy-done.2, s32[260]{0:T(512)} %subtract_select_fusion.blks, s32[72]{0:T(128)} %concatenate.3.lens, s32[2]{0:T(128)} %pad_add_fusion.meta, bf16[64,32,256]{2,1,0:T(8,128)(2,1)} %bitcast.17, bf16[64,1,256]{2,1,0:T(2,128)(2,1)} %copy.13.kn_ref, bf16[64,1,256]{2,1,0:T(2,128)(2,1)} %copy.14.vn_ref, ...), custom_call_target="tpu_custom_call" | custom-call | tf_op jit(solution)/shard_map/attend/pallas_call | solution.py:152
  112.9 1.3 slice.8
  114.2 1.6 copy.16
  115.8 82.6 %project_out.1 = bf16[8,64,8192]{2,1,0:T(8,128)(2,1)} custom-call(bf16[64,8192]{1,0:T(8,128)(2,1)} %bitcast.15, bf16[2048,4096]{1,0:T(8,128)(2,1)} %wo.1, bf16[8,64,8192]{2,1,0:T(8,128)(2,1)} %bitcast.14), custom_call_target="tpu_custom_call" | custom-call | tf_op jit(solution)/shard_map/project_out/pallas_call | solution.py:340
  198.4 0.0 copy-start.1
  198.4 0.0 copy-start
  198.4 7.8 %copy.20 = bf16[512,8192]{1,0:T(8,128)(2,1)} copy(bf16[512,8192]{1,0:T(8,128)(2,1)} %bitcast.13) | data formatting | bytes 16777216
  206.2 0.0 copy-done.1
  206.2 0.7 copy.21
  206.9 0.0 copy-done
  206.9 0.7 copy.22
Async XLA Ops:
  4.0 60.7 %copy-start.2 = (s32[260]{0:T(512)}, s32[260]{0:T(512)S(1)}, u32[]{:S(2)}) copy-start(s32[260]{0:T(512)S(1)} %get-tuple-element.10.seqs) | copy-start | bytes 3124
  198.4 7.9 %copy-start.1 = (bf16[512,256]{1,0:T(8,128)(2,1)S(1)}, bf16[512,256]{1,0:T(8,128)(2,1)}, u32[]{:S(2)}) copy-start(bf16[512,256]{1,0:T(8,128)(2,1)} %get-tuple-element.19) | copy-start | bytes 786436
  198.4 8.5 %copy-start = (bf16[512,256]{1,0:T(8,128)(2,1)S(1)}, bf16[512,256]{1,0:T(8,128)(2,1)}, u32[]{:S(2)}) copy-start(bf16[512,256]{1,0:T(8,128)(2,1)} %get-tuple-element.20) | copy-start | bytes 786436

commit v2 on v1

v2 whole, which is shorter than its diff:
```python
import functools

import jax
import jax.numpy as jnp
from jax import lax
from jax.experimental import pallas as pl
from jax.experimental.pallas import tpu as pltpu
from jax.sharding import PartitionSpec as P

MESH = pl.DeviceIdType.MESH
BK = 512
G = 4
RING = 6
AHEAD = 4
CH = 4
SUB = 4
NH = 8


def _vmem():
    return pl.BlockSpec(memory_space=pltpu.VMEM)


def _any():
    return pl.BlockSpec(memory_space=pl.ANY)


def _smem():
    return pl.BlockSpec(memory_space=pltpu.SMEM)


def _attn_kernel(scale, nm, lens, q_ref, kn_ref, vn_ref, kc, vc, o_ref, ko_ref, vo_ref,
                 seqs, blks, qa, qb, oa, ob, knf, vnf, kbuf, vbuf, pbuf, mbuf, lbuf, mrun, lrun, arun, ksem, vsem):
    nb = q_ref.shape[0]
    dh = kn_ref.shape[1]
    nh = q_ref.shape[1] // dh
    per = kc.shape[1] // BK
    start = (lax.axis_index("emb") * nm + lax.axis_index("model")) * nb

    def listed(sq, n):
        for t in range(per):
            seqs[n + t] = sq
            blks[n + t] = t
        return n + lens[start + sq] // BK + 1

    total = lax.fori_loop(0, nb, listed, 0, unroll=4)
    for t in range(G):
        seqs[total + t] = nb
        blks[total + t] = 0
    steps = (total + G - 1) // G

    def copies(g):
        slot = lax.rem(g, RING)
        out = []
        for u in range(G):
            n = g * G + u
            row = start + jnp.minimum(seqs[n], nb - 1)
            span = pl.ds(pl.multiple_of(blks[n] * BK, BK), BK)
            out.append((pltpu.make_async_copy(kc.at[row, span], kbuf.at[slot, u], ksem.at[slot, u]),
                        pltpu.make_async_copy(vc.at[row, span], vbuf.at[slot, u], vsem.at[slot, u])))
        return out

    def fetch(g):
        for ck, cv in copies(g):
            ck.start()
            cv.start()

    def landed(g, which):
        slot = lax.rem(g, RING)
        buf, sem, src = ((kbuf, ksem, kc), (vbuf, vsem, vc))[which]
        for u in range(G):
            pltpu.make_async_copy(src.at[0, pl.ds(0, BK)], buf.at[slot, u], sem.at[slot, u]).wait()

    def insert(buf, slot, u, row, new):
        base = pl.multiple_of(jnp.clip(row // 16, 0, BK // 16 - 1) * 16, 16)
        old = buf[slot, u, pl.ds(base, 16), :]
        at = lax.broadcasted_iota(jnp.int32, (16, 1), 0) + base == row
        buf[slot, u, pl.ds(base, 16), :] = jnp.where(at, new, old.astype(jnp.float32)).astype(jnp.bfloat16)

    def item(g, u):
        n = g * G + u
        seq = seqs[n]
        sq = jnp.minimum(seq, nb - 1)
        return seq, sq, blks[n], lens[start + sq] - blks[n] * BK

    def scores(g):
        slot = lax.rem(g, RING)
        half = lax.rem(g, 2)
        for u in range(G):
            _, sq, _, row = item(g, u)
            insert(kbuf, slot, u, row, knf[pl.ds(sq, 1), :])
            at = pl.ds(pl.multiple_of(sq * nh, nh), nh)
            qs = jnp.concatenate([qa[at, :], qb[at, :]], 1).astype(jnp.bfloat16)
            s = lax.dot_general(qs, kbuf[slot, u], (((1,), (1,)), ((), ())),
                                preferred_element_type=jnp.float32) * scale
            s = jnp.where(lax.broadcasted_iota(jnp.int32, s.shape, 1) <= row, s, -jnp.inf)
            m = jnp.max(s, axis=1, keepdims=True)
            p = jnp.exp(s - m)
            pbuf[half, u] = p.astype(jnp.bfloat16)
            mbuf[half, u] = jnp.broadcast_to(m, mbuf.shape[2:])
            lbuf[half, u] = jnp.broadcast_to(jnp.sum(p, axis=1, keepdims=True), lbuf.shape[2:])

    def values(g):
        slot = lax.rem(g, RING)
        half = lax.rem(g, 2)
        accs = []
        for u in range(G):
            _, sq, _, row = item(g, u)
            insert(vbuf, slot, u, row, vnf[pl.ds(sq, 1), :])
            accs.append(jnp.dot(pbuf[half, u], vbuf[slot, u], preferred_element_type=jnp.float32))
        mo, lo, ao = mrun[...], lrun[...], arun[...]
        for u in range(G):
            seq, _, blk, _ = item(g, u)
            first = blk == 0
            mo = jnp.where(first, -1e30, mo)
            lo = jnp.where(first, 0.0, lo)
            ao = jnp.where(first, 0.0, ao)
            m = jnp.maximum(mo, mbuf[half, u])
            alpha = jnp.exp(mo - m)
            beta = jnp.exp(mbuf[half, u] - m)
            lo = lo * alpha + lbuf[half, u] * beta
            ao = ao * jnp.concatenate([alpha, alpha], 1) + accs[u] * jnp.concatenate([beta, beta], 1)
            mo = m
            inv = 1.0 / lo
            at = pl.ds(pl.multiple_of(seq * nh, nh), nh)
            oa[at, :] = ao[:, :128] * inv
            ob[at, :] = ao[:, 128:] * inv
        mrun[...] = mo
        lrun[...] = lo
        arun[...] = ao

    for g in range(AHEAD + 1):
        @pl.when(g < steps)
        def _():
            fetch(g)

    mrun[...] = jnp.zeros_like(mrun)
    lrun[...] = jnp.zeros_like(lrun)
    arun[...] = jnp.zeros_like(arun)
    mine = pl.ds(pl.multiple_of(start, nb), nb)
    knf[...] = kn_ref[mine, :].astype(jnp.float32)
    vnf[...] = vn_ref[mine, :].astype(jnp.float32)
    for h in range(nh):
        qa[pl.ds(h, nb, stride=nh), :] = q_ref[:, h * dh:h * dh + 128].astype(jnp.float32)
        qb[pl.ds(h, nb, stride=nh), :] = q_ref[:, h * dh + 128:(h + 1) * dh].astype(jnp.float32)
    ko_ref[...] = kn_ref[...]
    vo_ref[...] = vn_ref[...]

    landed(0, 0)
    scores(0)

    def body(g, c):
        @pl.when(g + AHEAD < steps)
        def _():
            fetch(g + AHEAD)

        landed(g - 1, 1)
        landed(g, 0)
        values(g - 1)
        scores(g)
        return c

    lax.fori_loop(1, steps, body, 0)
    landed(steps - 1, 1)
    values(steps - 1)
    for h in range(nh):
        o_ref[:, h * dh:h * dh + 128] = oa[pl.ds(h, nb, stride=nh), :].astype(jnp.bfloat16)
        o_ref[:, h * dh + 128:(h + 1) * dh] = ob[pl.ds(h, nb, stride=nh), :].astype(jnp.bfloat16)


def _attend(q, k_new, v_new, Kc, Vc, lengths, nm):
    nb, full = q.shape
    t, dh = Kc.shape[1:]
    h = full // dh
    assert dh == 256 and t % BK == 0
    most = nb * (t // BK) + 2 * G
    bf, f32 = jnp.bfloat16, jnp.float32
    kv = jax.ShapeDtypeStruct(k_new.shape, bf)
    return pl.pallas_call(
        functools.partial(_attn_kernel, dh ** -0.5, nm),
        out_shape=(jax.ShapeDtypeStruct((nb, full), bf), kv, kv),
        in_specs=[_smem()] + [_vmem()] * 3 + [_any()] * 2,
        out_specs=(_vmem(), _vmem(), _vmem()),
        scratch_shapes=[
            pltpu.SMEM((most,), jnp.int32), pltpu.SMEM((most,), jnp.int32),
            pltpu.VMEM((nb * h, 128), f32), pltpu.VMEM((nb * h, 128), f32),
            pltpu.VMEM((nb * h + h, 128), f32), pltpu.VMEM((nb * h + h, 128), f32),
            pltpu.VMEM((nb, dh), f32), pltpu.VMEM((nb, dh), f32),
            pltpu.VMEM((RING, G, BK, dh), bf), pltpu.VMEM((RING, G, BK, dh), bf),
            pltpu.VMEM((2, G, h, BK), bf), pltpu.VMEM((2, G, h, 128), f32), pltpu.VMEM((2, G, h, 128), f32),
            pltpu.VMEM((h, 128), f32), pltpu.VMEM((h, 128), f32), pltpu.VMEM((h, dh), f32),
            pltpu.SemaphoreType.DMA((RING, G)), pltpu.SemaphoreType.DMA((RING, G)),
        ],
        compiler_params=pltpu.CompilerParams(vmem_limit_bytes=40 << 20),
        name="attend",
    )(lengths, q, k_new, v_new, Kc, Vc)


def _out_kernel(ne, nm, o_ref, wo, x, y, wv, xv, ob, pown, psend, precv, ssend, srecv,
                wsem, xsem, osend, orecv, vsend, vrecv, ps, pr, xs_, xr, cs, cr, es, er, fs, fr):
    i = lax.axis_index("emb")
    j = lax.axis_index("model")
    c = lax.rem(j, 2)
    jp = j + 1 - 2 * c
    jx = lax.rem(j + 2, nm)
    ie = 1 - i
    half = wv.shape[2]
    cw = half // SUB
    rows = o_ref.shape[0] // CH
    kk = wv.shape[1]
    dev = ne * nm

    def at(a, b):
        return {"emb": a, "model": b}

    def wcopy(b, u):
        col = pl.multiple_of((1 - c if b == 0 else c) * half + u * cw, cw)
        return pltpu.make_async_copy(wo.at[:, pl.ds(col, cw)], wv.at[b, :, pl.ds(u * cw, cw)], wsem.at[b, u])

    for b in range(2):
        for u in range(SUB):
            wcopy(b, u).start()
    mycol = pl.multiple_of((i * 2 + c) * half, half)
    excol = pl.multiple_of((ie * 2 + c) * half, half)
    xcopy = pltpu.make_async_copy(x.at[:, :, pl.ds(mycol, half)], xv, xsem)
    xcopy.start()

    barrier = pltpu.get_barrier_semaphore()
    pl.semaphore_signal(barrier, inc=1, device_id=at(ie, j), device_id_type=MESH)
    for r in range(1, nm):
        pl.semaphore_signal(barrier, inc=1, device_id=at(i, lax.rem(j + r, nm)), device_id_type=MESH)
    pl.semaphore_wait(barrier, nm)

    def ocopy(s, r):
        d = lax.rem(j + r, nm)
        return pltpu.make_async_remote_copy(
            src_ref=o_ref.at[pl.ds(s * rows, rows), pl.ds(pl.multiple_of(d * kk, kk), kk)],
            dst_ref=ob.at[s, pl.ds(pl.multiple_of((i * nm + j) * rows, rows), rows), :],
            send_sem=osend.at[s, r], recv_sem=orecv.at[s, nm - r],
            device_id=at(i, d), device_id_type=MESH)

    def orecv_copy(s, r):
        d = lax.rem(j + r, nm)
        blk = ob.at[s, pl.ds(pl.multiple_of((i * nm + d) * rows, rows), rows), :]
        return pltpu.make_async_remote_copy(
            src_ref=blk, dst_ref=blk, send_sem=osend.at[s, r], recv_sem=orecv.at[s, r],
            device_id=at(i, d), device_id_type=MESH)

    def vcopy(s, r):
        dst = ob.at[s, pl.ds(pl.multiple_of((i * nm + lax.rem(j + r, nm)) * rows, rows), rows), :]
        src = o_ref.at[pl.ds(s * rows, rows), pl.ds(pl.multiple_of(j * kk, kk), kk)] if r == 0 else dst
        return pltpu.make_async_remote_copy(
            src_ref=src, dst_ref=dst, send_sem=vsend.at[s, r], recv_sem=vrecv.at[s, r],
            device_id=at(ie, j), device_id_type=MESH)

    def vrecv_copy(s, r):
        blk = ob.at[s, pl.ds(pl.multiple_of((ie * nm + lax.rem(j + r, nm)) * rows, rows), rows), :]
        return pltpu.make_async_remote_copy(
            src_ref=blk, dst_ref=blk, send_sem=vsend.at[s, r], recv_sem=vrecv.at[s, r],
            device_id=at(ie, j), device_id_type=MESH)

    for s in range(CH):
        for r in (2, 3, 1):
            ocopy(s, r).start()
    vcopy(0, 0).start()
    for s in range(CH):
        ob[s, pl.ds(pl.multiple_of((i * nm + j) * rows, rows), rows), :] = o_ref[
            pl.ds(s * rows, rows), pl.ds(pl.multiple_of(j * kk, kk), kk)]

    def relay(s):
        for r in (1, 2, 3):
            orecv_copy(s, r).wait_recv()
            vcopy(s, r).start()

    relay(0)
    vcopy(1, 0).start()
    relay(1)

    def pcopy(s, u):
        return pltpu.make_async_remote_copy(
            src_ref=psend.at[s, u], dst_ref=precv.at[s, u], send_sem=ps.at[s, u], recv_sem=pr.at[s, u],
            device_id=at(i, jp), device_id_type=MESH)

    def scopy(s, u):
        return pltpu.make_async_remote_copy(
            src_ref=ssend.at[s, u], dst_ref=srecv.at[s, u], send_sem=xs_.at[s, u], recv_sem=xr.at[s, u],
            device_id=at(i, jx), device_id_type=MESH)

    def piece(s, u, base):
        return y.at[:, pl.ds(pl.multiple_of(s * rows, rows), rows), pl.ds(pl.multiple_of(base + u * cw, cw), cw)]

    def ccopy(s, u):
        return pltpu.make_async_remote_copy(
            src_ref=piece(s, u, mycol), dst_ref=piece(s, u, mycol), send_sem=cs.at[s, u], recv_sem=cr.at[s, u],
            device_id=at(i, jp), device_id_type=MESH)

    def ecopy(s, u):
        return pltpu.make_async_remote_copy(
            src_ref=piece(s, u, mycol), dst_ref=piece(s, u, mycol), send_sem=es.at[s, u], recv_sem=er.at[s, u],
            device_id=at(ie, j), device_id_type=MESH)

    def fcopy(s, u):
        return pltpu.make_async_remote_copy(
            src_ref=piece(s, u, excol), dst_ref=piece(s, u, excol), send_sem=fs.at[s, u], recv_sem=fr.at[s, u],
            device_id=at(i, jp), device_id_type=MESH)

    for b in range(2):
        for u in range(SUB):
            wcopy(b, u).wait()
    xcopy.wait()

    def compute(s):
        for r in range(nm):
            vrecv_copy(s, r).wait_recv()
        lhs = ob[s]
        for u in range(SUB):
            psend[s, u] = jnp.dot(lhs, wv[0, :, u * cw:(u + 1) * cw],
                                  preferred_element_type=jnp.float32).astype(jnp.bfloat16)
            pcopy(s, u).start()
        for u in range(SUB):
            pown[u] = jnp.dot(lhs, wv[1, :, u * cw:(u + 1) * cw], preferred_element_type=jnp.float32)
            pcopy(s, u).wait_recv()
            ssend[s, u] = (pown[u] + precv[s, u].astype(jnp.float32)).astype(jnp.bfloat16)
            scopy(s, u).start()

    def finish(s):
        at_rows = pl.ds(pl.multiple_of(s * rows, rows), rows)
        for u in range(SUB):
            scopy(s, u).wait_recv()
            tot = ssend[s, u].astype(jnp.float32) + srecv[s, u].astype(jnp.float32)
            xs = xv[:, at_rows, u * cw:(u + 1) * cw].astype(jnp.float32)
            y[:, at_rows, pl.ds(pl.multiple_of(mycol + u * cw, cw), cw)] = (
                xs + tot.reshape(dev, rows, cw)).astype(jnp.bfloat16)
            ecopy(s, u).start()
            ccopy(s, u).start()

    def forward(s):
        for u in range(SUB):
            ecopy(s, u).wait_recv()
            fcopy(s, u).start()

    def step(s, carry):
        compute(s)

        @pl.when(s + 2 < CH)
        def _():
            vcopy_late(s + 2)

        @pl.when(s >= 1)
        def _():
            finish(s - 1)

        @pl.when(s >= 2)
        def _():
            forward(s - 2)

        return carry

    def vcopy_late(s):
        at_rows = pl.ds(pl.multiple_of(s * rows, rows), rows)
        own = pl.ds(pl.multiple_of((i * nm + j) * rows, rows), rows)
        pltpu.make_async_remote_copy(
            src_ref=o_ref.at[at_rows, pl.ds(pl.multiple_of(j * kk, kk), kk)], dst_ref=ob.at[s, own, :],
            send_sem=vsend.at[s, 0], recv_sem=vrecv.at[s, 0], device_id=at(ie, j), device_id_type=MESH).start()
        relay(s)

    lax.fori_loop(0, CH, step, 0)
    finish(CH - 1)
    forward(CH - 2)
    forward(CH - 1)
    for s in range(CH):
        for r in range(1, nm):
            ocopy(s, r).wait_send()
        for r in range(nm):
            vcopy(s, r).wait_send()
        for u in range(SUB):
            pcopy(s, u).wait_send()
            scopy(s, u).wait_send()
            ecopy(s, u).wait_send()
            ccopy(s, u).wait()
            fcopy(s, u).wait()


def _project_out(o, Wo, x, ne, nm):
    bl, full = o.shape
    kk, ncol = Wo.shape
    half = ncol // 2
    dev = ne * nm
    rows = bl // CH
    cw = half // SUB
    b, d = x.shape
    bf, f32 = jnp.bfloat16, jnp.float32
    dma = pltpu.SemaphoreType.DMA
    pieces = pltpu.VMEM((CH, SUB, dev * rows, cw), bf)
    y = pl.pallas_call(
        functools.partial(_out_kernel, ne, nm),
        out_shape=pltpu.VMEM((dev, bl, d), bf),
        in_specs=[_vmem(), _any(), _any()],
        out_specs=_vmem(),
        scratch_shapes=[
            pltpu.VMEM((2, kk, half), bf), pltpu.VMEM((dev, bl, half), bf), pltpu.VMEM((CH, dev * rows, kk), bf),
            pltpu.VMEM((SUB, dev * rows, cw), f32), pieces, pieces, pieces, pieces,
            dma((2, SUB)), dma,
        ] + [dma((CH, nm))] * 4 + [dma((CH, SUB))] * 10,
        compiler_params=pltpu.CompilerParams(collective_id=1, has_side_effects=True, vmem_limit_bytes=36 << 20),
        name="project_out",
    )(o, Wo, x.reshape(dev, bl, d))
    return y.reshape(b, d)


def _in_kernel(ne, nm, x, wq, wk, wv, q, k_out, v_out, xv, wqv, wkv, qsend, qrecv, qown, qb,
               xsem, wsem, ksem, ss, sr, hs, hr, ls):
    i = lax.axis_index("emb")
    j = lax.axis_index("model")
    ie = 1 - i
    de = wq.shape[0]
    be = xv.shape[1] // 2
    bl = be // nm
    cw = wq.shape[1] // NH
    dh = wk.shape[1]

    def at(a, b):
        return {"emb": a, "model": b}

    def xcopy(a, r):
        row = pl.multiple_of((ie if a == 0 else i) * be, be)
        col = pl.multiple_of((i if r == 0 else ie) * de, de)
        return pltpu.make_async_copy(x.at[pl.ds(row, be), pl.ds(col, de)], xv.at[r, a * be:(a + 1) * be, :], xsem.at[a, r])

    def wcopy(h):
        return pltpu.make_async_copy(wq.at[:, pl.ds(h * cw, cw)], wqv.at[h], wsem.at[h])

    def kcopy(n, r):
        src = wk if n == 0 else wv
        row = pl.multiple_of((i if r == 0 else ie) * de, de)
        return pltpu.make_async_copy(src.at[pl.ds(row, de), :], wkv.at[n, r], ksem.at[n, r])

    xcopy(0, 0).start()
    for h in range(NH):
        wcopy(h).start()
    xcopy(1, 0).start()
    xcopy(0, 1).start()
    xcopy(1, 1).start()
    for n in range(2):
        for r in range(2):
            kcopy(n, r).start()

    barrier = pltpu.get_barrier_semaphore()
    pl.semaphore_signal(barrier, inc=1, device_id=at(ie, j), device_id_type=MESH)
    for r in range(1, nm):
        pl.semaphore_signal(barrier, inc=1, device_id=at(i, lax.rem(j + r, nm)), device_id_type=MESH)
    pl.semaphore_wait(barrier, nm)

    def scopy(h):
        return pltpu.make_async_remote_copy(
            src_ref=qsend.at[h], dst_ref=qrecv.at[h], send_sem=ss.at[h], recv_sem=sr.at[h],
            device_id=at(ie, j), device_id_type=MESH)

    def hcopy(h, r):
        d = lax.rem(j + r, nm)
        return pltpu.make_async_remote_copy(
            src_ref=qb.at[h, pl.ds(pl.multiple_of(d * bl, bl), bl), :],
            dst_ref=q.at[:, pl.ds(pl.multiple_of((j * NH + h) * cw, cw), cw)],
            send_sem=hs.at[h, r], recv_sem=hr.at[h, nm - r],
            device_id=at(i, d), device_id_type=MESH)

    def hrecv(h, r):
        d = lax.rem(j + r, nm)
        return pltpu.make_async_remote_copy(
            src_ref=qb.at[h, pl.ds(0, bl), :],
            dst_ref=q.at[:, pl.ds(pl.multiple_of((d * NH + h) * cw, cw), cw)],
            send_sem=hs.at[h, r], recv_sem=hr.at[h, r],
            device_id=at(i, d), device_id_type=MESH)

    def hself(h):
        return pltpu.make_async_copy(
            qb.at[h, pl.ds(pl.multiple_of(j * bl, bl), bl), :],
            q.at[:, pl.ds(pl.multiple_of((j * NH + h) * cw, cw), cw)], ls.at[h])

    xcopy(0, 0).wait()
    for h in range(NH):
        wcopy(h).wait()
        qsend[h] = jnp.dot(xv[0, :be, :], wqv[h], preferred_element_type=jnp.float32)
        scopy(h).start()
    xcopy(1, 0).wait()
    for h in range(NH):
        qown[h] = jnp.dot(xv[0, be:, :], wqv[h], preferred_element_type=jnp.float32)

    xcopy(0, 1).wait()
    xcopy(1, 1).wait()
    for n in range(2):
        for r in range(2):
            kcopy(n, r).wait()
    for n, out in ((0, k_out), (1, v_out)):
        for a in range(2):
            acc = jnp.dot(xv[0, a * be:(a + 1) * be, :], wkv[n, 0], preferred_element_type=jnp.float32)
            acc += jnp.dot(xv[1, a * be:(a + 1) * be, :], wkv[n, 1], preferred_element_type=jnp.float32)
            out[pl.ds(pl.multiple_of((ie if a == 0 else i) * be, be), be), :] = acc.astype(jnp.bfloat16)

    for h in range(NH):
        scopy(h).wait_recv()
        qb[h] = (qown[h] + qrecv[h]).astype(jnp.bfloat16)
        for r in (2, 3, 1):
            hcopy(h, r).start()
        hself(h).start()
    for h in range(NH):
        scopy(h).wait_send()
        hself(h).wait()
        for r in range(1, nm):
            hcopy(h, r).wait_send()
            hrecv(h, r).wait_recv()


def _project_in(x, Wq, Wk, Wv, ne, nm):
    b, d = x.shape
    de, hw = Wq.shape
    dh = Wk.shape[1]
    be = b // ne
    bl = be // nm
    cw = hw // NH
    bf, f32 = jnp.bfloat16, jnp.float32
    dma = pltpu.SemaphoreType.DMA
    return pl.pallas_call(
        functools.partial(_in_kernel, ne, nm),
        out_shape=(jax.ShapeDtypeStruct((bl, hw * nm), bf), jax.ShapeDtypeStruct((b, dh), bf),
                   jax.ShapeDtypeStruct((b, dh), bf)),
        in_specs=[_any()] * 4,
        out_specs=(_any(), _vmem(), _vmem()),
        scratch_shapes=[
            pltpu.VMEM((2, b, de), bf), pltpu.VMEM((NH, de, cw), bf), pltpu.VMEM((2, 2, de, dh), bf),
            pltpu.VMEM((NH, be, cw), f32), pltpu.VMEM((NH, be, cw), f32), pltpu.VMEM((NH, be, cw), f32),
            pltpu.VMEM((NH, be, cw), bf),
            dma((2, 2)), dma((NH,)), dma((2, 2)), dma((NH,)), dma((NH,)), dma((NH, nm)), dma((NH, nm)), dma((NH,)),
        ],
        compiler_params=pltpu.CompilerParams(collective_id=0, has_side_effects=True, vmem_limit_bytes=60 << 20),
        name="project_in",
    )(x, Wq, Wk, Wv)


def solution(mesh):
    ne = mesh.shape['emb']
    nm = mesh.shape['model']

    def local(x, Wq, Wk, Wv, Wo, Kc, Vc, lengths):
        q, k_new, v_new = _project_in(x, Wq, Wk, Wv, ne, nm)
        o, k_new, v_new = _attend(q, k_new, v_new, Kc, Vc, lengths, nm)
        y = _project_out(o, Wo, x, ne, nm)
        return y, k_new, v_new

    in_specs = (P('rep', None), P('emb', 'model'), P(), P(), P('model', 'emb'),
                P('rep', None, None), P('rep', None, None), P('rep'))
    out_specs = (P('rep', None), P('rep', None), P('rep', None))
    return jax.shard_map(local, mesh=mesh, in_specs=in_specs, out_specs=out_specs, check_vma=False)
```

time: 207 us -> 183 us (0.88)
  local copies, waits for them, and re-layouts: 17.9 us -> 6.52 us
  Pallas kernels: 186 us -> 176 us
  other arithmetic: 2.11 us -> 0 us
    pallas_call x2, Pallas kernels: 126 us -> 115 us  [the longest x1 80 us: _project_out(): pl.pallas_call(functools.partial(_out_kernel, ne, nm), out_shape=pltpu.VM...]
    unnamed x11, local copies, waits for them, and re-layouts: 13.3 us -> 6.52 us
    reshape x3 -> x0, local copies, waits for them, and re-layouts: 2.14 us -> none  [the longest x2 1.46 us: _attend(): vn.reshape(nb, 1, dh)]
where the time goes in v2:
time: 183 us
  Pallas kernels  176 us (96%)
  local copies, waits for them, and re-layouts  6.52 us (4%)
    pallas_call x1, Pallas kernels, _project_out(): pl.pallas_call(functools.partial(_out_kernel, ne, nm), out_shape=pltpu.VM...  80 us
    pallas_call x1, Pallas kernels, _project_in(): pl.pallas_call(functools.partial(_in_kernel, ne, nm), out_shape=(jax.Shap...  60.3 us
    pallas_call x1, Pallas kernels, _attend(): pl.pallas_call(functools.partial(_attn_kernel, dh ** (-0.5), nm), out_sha...  35.3 us
    unnamed x11, local copies, waits for them, and re-layouts  6.52 us

profile of v2, /device:TPU:0, one launch (start us, length us, event | category | flops | bytes accessed | tf_op | source)
XLA Modules:
  0.0 182.8 jit_solution(6088655101342762111)
XLA Ops:
  0.6 0.0 copy-start.4
  0.6 60.3 %project_in.1 = (bf16[64,8192]{1,0:T(8,128)(2,1)}, bf16[512,256]{1,0:T(8,128)(2,1)}, bf16[512,256]{1,0:T(8,128)(2,1)}) custom-call(bf16[512,8192]{1,0:T(8,128)(2,1)} %x.1, bf16[4096,2048]{1,0:T(8,128)(2,1)} %wq.1, bf16[8192,256]{1,0:T(8,128)(2,1)} %wk.1, bf16[8192,256]{1,0:T(8,128)(2,1)} %wv.1), custom_call_target="tpu_custom_call" | custom-call | tf_op jit(solution)/shard_map/project_in/pallas_call | solution.py:523
  60.9 0.0 copy-done.4
  61.0 0.0 copy-start.1
  61.0 1.2 copy-done.1
  62.2 0.0 copy-start.2
  62.2 0.9 copy-done.2
  63.1 0.0 copy-start.3
  63.1 0.9 copy-done.3
  64.1 0.0 copy-start
  64.1 35.3 %attend.1 = (bf16[64,8192]{1,0:T(8,128)(2,1)S(1)}, bf16[512,256]{1,0:T(8,128)(2,1)}, bf16[512,256]{1,0:T(8,128)(2,1)}) custom-call(s32[512]{0:T(512)S(1)} %copy-done.4, bf16[64,8192]{1,0:T(8,128)(2,1)S(1)} %copy-done.1, bf16[512,256]{1,0:T(8,128)(2,1)S(1)} %copy-done.2, bf16[512,256]{1,0:T(8,128)(2,1)S(1)} %copy-done.3, bf16[512,2048,256]{2,1,0:T(8,128)(2,1)} %kc.1, ...), custom_call_target="tpu_custom_call" | custom-call | tf_op jit(solution)/shard_map/attend/pallas_call | solution.py:179
  99.4 0.0 copy-done
  99.4 80.0 %project_out.1 = bf16[8,64,8192]{2,1,0:T(8,128)(2,1)S(1)} custom-call(bf16[64,8192]{1,0:T(8,128)(2,1)S(1)} %get-tuple-element.12.o_ref, bf16[2048,4096]{1,0:T(8,128)(2,1)} %wo.1, bf16[8,64,8192]{2,1,0:T(8,128)(2,1)S(1)} %bitcast.3), custom_call_target="tpu_custom_call" | custom-call | tf_op jit(solution)/shard_map/project_out/pallas_call | solution.py:395
  179.4 3.4 %copy.12 = bf16[512,8192]{1,0:T(8,128)(2,1)} copy(bf16[512,8192]{1,0:T(8,128)(2,1)S(1)} %bitcast.2) | data formatting | bytes 16777216
Async XLA Ops:
  0.6 60.3 %copy-start.4 = (s32[512]{0:T(512)S(1)}, s32[512]{0:T(512)}, u32[]{:S(2)}) copy-start(s32[512]{0:T(512)} %lens.1) | copy-start | bytes 6148
  61.0 1.2 copy-start.1
  62.2 0.9 copy-start.2
  63.1 0.9 copy-start.3
  64.1 35.3 %copy-start = (bf16[512,8192]{1,0:T(8,128)(2,1)S(1)}, bf16[512,8192]{1,0:T(8,128)(2,1)}, u32[]{:S(2)}) copy-start(bf16[512,8192]{1,0:T(8,128)(2,1)} %x.1) | copy-start | bytes 25165828

commit v3 on v0

v3 whole, which is shorter than its diff:
```python
import functools

import jax
import jax.numpy as jnp
from jax import lax
from jax.experimental import pallas as pl
from jax.experimental.pallas import tpu as pltpu
from jax.sharding import PartitionSpec as P

MESH = pl.DeviceIdType.MESH
BK = 512
HOOK = 3
VLIM = 60
RING = 6
CH = 4
SUB = 4
NH = 8


def _vmem():
    return pl.BlockSpec(memory_space=pltpu.VMEM)


def _hbm():
    return pl.BlockSpec(memory_space=pltpu.HBM)


def _smem():
    return pl.BlockSpec(memory_space=pltpu.SMEM)


def _qa_kernel(ne, nm, scale, lens, x, wq, wk, wv, kc, vc, ob, olast, k_out, v_out,
               xv, wqv, wkv, qsend, qrecv, qown, qc, qin, qa, qb, oa, obh, ost, knf, vnf, kbuf, vbuf,
               sa, sb, ma, mb, na, nb_,
               xsem, wsem, kvsem, ss0, sr0, ss, sr, hs, hr, osend, orecv, vsend, vrecv, ksem, vsem):
    i = lax.axis_index("emb")
    j = lax.axis_index("model")
    ie = 1 - i
    de = wq.shape[0]
    be = xv.shape[1] // 2
    bl = be // nm
    rows = bl // CH
    kk = wq.shape[1]
    cw = kk // NH
    dh = wk.shape[1]
    nh = ost.shape[2] // dh
    slots = kc.shape[1]
    start = i * be + j * bl

    def at(a, b):
        return {"emb": a, "model": b}

    def xcopy(a, r):
        row = pl.multiple_of((ie if a == 0 else i) * be, be)
        col = pl.multiple_of((i if r == 0 else ie) * de, de)
        return pltpu.make_async_copy(x.at[pl.ds(row, be), pl.ds(col, de)], xv.at[r, a * be:(a + 1) * be, :], xsem.at[a, r])

    def wcopy(h):
        return pltpu.make_async_copy(wq.at[:, pl.ds(h * cw, cw)], wqv.at[h], wsem.at[h])

    def kvcopy(n, r):
        src = wk if n == 0 else wv
        row = pl.multiple_of((i if r == 0 else ie) * de, de)
        return pltpu.make_async_copy(src.at[pl.ds(row, de), :], wkv.at[n, r], kvsem.at[n, r])

    def kcopy(n):
        slot = lax.rem(n, RING)
        return pltpu.make_async_copy(kc.at[start + n], kbuf.at[slot], ksem.at[slot])

    def vcopy(n):
        slot = lax.rem(n, RING)
        return pltpu.make_async_copy(vc.at[start + n], vbuf.at[slot], vsem.at[slot])

    xcopy(0, 0).start()
    for h in range(NH):
        wcopy(h).start()
    xcopy(1, 0).start()
    xcopy(0, 1).start()
    xcopy(1, 1).start()
    for n in range(2):
        for r in range(2):
            kvcopy(n, r).start()
    for n in range(RING - 1):
        kcopy(n).start()
        if n < RING - 2:
            vcopy(n).start()

    barrier = pltpu.get_barrier_semaphore()
    pl.semaphore_signal(barrier, inc=1, device_id=at(ie, j), device_id_type=MESH)
    for r in range(1, nm):
        pl.semaphore_signal(barrier, inc=1, device_id=at(i, lax.rem(j + r, nm)), device_id_type=MESH)
    pl.semaphore_wait(barrier, nm)

    def first(h):
        return pltpu.make_async_remote_copy(
            src_ref=qsend.at[0, :, pl.ds(h * cw, cw)], dst_ref=qrecv.at[0, :, pl.ds(h * cw, cw)],
            send_sem=ss0.at[h], recv_sem=sr0.at[h], device_id=at(ie, j), device_id_type=MESH)

    def later(s):
        return pltpu.make_async_remote_copy(
            src_ref=qsend.at[s], dst_ref=qrecv.at[s], send_sem=ss.at[s], recv_sem=sr.at[s],
            device_id=at(ie, j), device_id_type=MESH)

    def mycols(d):
        return pl.ds(pl.multiple_of(d * kk, kk), kk)

    def hcopy(s, r):
        d = lax.rem(j + r, nm)
        return pltpu.make_async_remote_copy(
            src_ref=qc.at[s, pl.ds(pl.multiple_of(d * rows, rows), rows), :], dst_ref=qin.at[s, :, mycols(j)],
            send_sem=hs.at[s, r], recv_sem=hr.at[s, nm - r], device_id=at(i, d), device_id_type=MESH)

    def hrecv(s, r):
        d = lax.rem(j + r, nm)
        return pltpu.make_async_remote_copy(
            src_ref=qc.at[s, pl.ds(0, rows), :], dst_ref=qin.at[s, :, mycols(d)],
            send_sem=hs.at[s, r], recv_sem=hr.at[s, r], device_id=at(i, d), device_id_type=MESH)

    def block(a, d):
        return pl.ds(pl.multiple_of((a * nm + d) * rows, rows), rows)

    def ocopy(s, r):
        d = lax.rem(j + r, nm)
        return pltpu.make_async_remote_copy(
            src_ref=ost.at[s, :, mycols(d)], dst_ref=ob.at[s, block(i, j), :],
            send_sem=osend.at[s, r], recv_sem=orecv.at[s, nm - r], device_id=at(i, d), device_id_type=MESH)

    def orecv_copy(s, r):
        d = lax.rem(j + r, nm)
        return pltpu.make_async_remote_copy(
            src_ref=ob.at[s, block(i, d), :], dst_ref=ob.at[s, block(i, d), :],
            send_sem=osend.at[s, r], recv_sem=orecv.at[s, r], device_id=at(i, d), device_id_type=MESH)

    def ycopy(s, r):
        dst = ob.at[s, block(i, lax.rem(j + r, nm)), :]
        return pltpu.make_async_remote_copy(
            src_ref=ost.at[s, :, mycols(j)] if r == 0 else dst, dst_ref=dst,
            send_sem=vsend.at[s, r], recv_sem=vrecv.at[s, r], device_id=at(ie, j), device_id_type=MESH)

    def yrecv_copy(s, r):
        blk = ob.at[s, block(ie, lax.rem(j + r, nm)), :]
        return pltpu.make_async_remote_copy(
            src_ref=blk, dst_ref=blk, send_sem=vsend.at[s, r], recv_sem=vrecv.at[s, r],
            device_id=at(ie, j), device_id_type=MESH)

    def spread(dst, h, val):
        for s in range(CH):
            for d in range(nm):
                dst[s, d * rows:(d + 1) * rows, h * cw:(h + 1) * cw] = val[d * bl + s * rows:d * bl + (s + 1) * rows]

    xcopy(0, 0).wait()
    for h in range(NH):
        wcopy(h).wait()
        spread(qsend, h, jnp.dot(xv[0, :be, :], wqv[h], preferred_element_type=jnp.float32))
        first(h).start()
    for s in range(1, CH):
        later(s).start()
    xcopy(1, 0).wait()
    for h in range(NH):
        spread(qown, h, jnp.dot(xv[0, be:, :], wqv[h], preferred_element_type=jnp.float32))
    xcopy(0, 1).wait()
    xcopy(1, 1).wait()
    for n in range(2):
        for r in range(2):
            kvcopy(n, r).wait()
    for n, out, rowf in ((0, k_out, knf), (1, v_out, vnf)):
        for a in range(2):
            acc = jnp.dot(xv[0, a * be:(a + 1) * be, :], wkv[n, 0], preferred_element_type=jnp.float32)
            acc += jnp.dot(xv[1, a * be:(a + 1) * be, :], wkv[n, 1], preferred_element_type=jnp.float32)
            out[pl.ds(pl.multiple_of((ie if a == 0 else i) * be, be), be), :] = acc.astype(jnp.bfloat16)
        rowf[...] = out[pl.ds(pl.multiple_of(start, bl), bl), :].astype(jnp.float32)

    def deal(s):
        qc[s] = (qown[s] + qrecv[s]).astype(jnp.bfloat16)
        for r in (2, 3, 1):
            hcopy(s, r).start()
        qin[s, :, mycols(j)] = qc[s, pl.ds(pl.multiple_of(j * rows, rows), rows), :]

    def relay(s):
        for r in range(1, nm):
            orecv_copy(s, r).wait_recv()
            ycopy(s, r).start()

    for h in range(NH):
        first(h).wait_recv()
    deal(0)

    def scores(s, n, sref, mref, nref):
        t = n - s * rows
        seq = pl.ds(pl.multiple_of(t * nh, nh), nh)
        qf = jnp.concatenate([qa[seq, :], qb[seq, :]], 1)
        q = qf.astype(jnp.bfloat16)
        slot = lax.rem(n, RING)
        new = jnp.sum(qf * knf[pl.ds(n, 1), :], axis=1, keepdims=True) * scale
        count = lens[start + n]
        top = None
        for b in range(slots // BK):
            v = lax.dot_general(q, kbuf[slot, b * BK:(b + 1) * BK, :], (((1,), (1,)), ((), ())),
                                preferred_element_type=jnp.float32) * scale
            v = jnp.where(lax.broadcasted_iota(jnp.int32, v.shape, 1) + b * BK < count, v, -jnp.inf)
            sref[:, b * BK:(b + 1) * BK] = v
            top = v if top is None else jnp.maximum(top, v)
        m = jnp.maximum(jnp.max(top, axis=1, keepdims=True), new)
        mref[...] = jnp.broadcast_to(m, mref.shape)
        nref[...] = jnp.broadcast_to(new, nref.shape)

    def values(s, n, sref, mref, nref):
        t = n - s * rows
        seq = pl.ds(pl.multiple_of(t * nh, nh), nh)
        slot = lax.rem(n, RING)
        m = mref[...]
        wide = jnp.concatenate([m] * (BK // 128), 1)
        ps, tot = [], None
        for b in range(slots // BK):
            p = jnp.exp(sref[:, b * BK:(b + 1) * BK] - wide)
            tot = p if tot is None else tot + p
            ps.append(p.astype(jnp.bfloat16))
        acc = jnp.dot(jnp.concatenate(ps, 1), vbuf[slot], preferred_element_type=jnp.float32)
        pn = jnp.exp(nref[...] - m)
        inv = 1.0 / (jnp.sum(tot, axis=1, keepdims=True) + pn)
        pn = pn.astype(jnp.bfloat16).astype(jnp.float32)
        vn = vnf[pl.ds(n, 1), :]
        oa[seq, :] = (acc[:, :128] + pn * vn[:, :128]) * inv
        obh[seq, :] = (acc[:, 128:] + pn * vn[:, 128:]) * inv

    A, B = (sa, ma, na), (sb, mb, nb_)

    def fetch(n):
        @pl.when(n + RING - 1 < bl)
        def _():
            kcopy(n + RING - 1).start()
            vcopy(n + RING - 2).start()

        @pl.when(n + RING - 1 == bl)
        def _():
            vcopy(n + RING - 2).start()

        @pl.when(n + RING < bl)
        def _():
            kcopy(n + RING).start()
            vcopy(n + RING - 1).start()

        @pl.when(n + RING == bl)
        def _():
            vcopy(n + RING - 1).start()

    def chunk(s, carry):
        n0 = s * rows
        for r in range(1, nm):
            hrecv(s, r).wait_recv()
        for h in range(nh):
            qa[pl.ds(h, rows, stride=nh), :] = qin[s, :, h * dh:h * dh + 128].astype(jnp.float32)
            qb[pl.ds(h, rows, stride=nh), :] = qin[s, :, h * dh + 128:(h + 1) * dh].astype(jnp.float32)
        kcopy(n0).wait()
        scores(s, n0, *A)

        def pair(t, c):
            n = n0 + 2 * t

            @pl.when(t == HOOK)
            def _():
                @pl.when(s + 1 < CH)
                def _():
                    later(s + 1).wait_recv()
                    deal(s + 1)

                @pl.when(s >= 1)
                def _():
                    relay(s - 1)

            fetch(n)
            kcopy(n + 1).wait()
            vcopy(n).wait()
            values(s, n, *A)
            scores(s, n + 1, *B)
            kcopy(n + 2).wait()
            vcopy(n + 1).wait()
            values(s, n + 1, *B)
            scores(s, n + 2, *A)
            return c

        lax.fori_loop(0, rows // 2 - 1, pair, 0)
        n = n0 + rows - 2
        fetch(n)
        kcopy(n + 1).wait()
        vcopy(n).wait()
        values(s, n, *A)
        scores(s, n + 1, *B)
        vcopy(n + 1).wait()
        values(s, n + 1, *B)
        for h in range(nh):
            ost[s, :, h * dh:h * dh + 128] = oa[pl.ds(h, rows, stride=nh), :].astype(jnp.bfloat16)
            ost[s, :, h * dh + 128:(h + 1) * dh] = obh[pl.ds(h, rows, stride=nh), :].astype(jnp.bfloat16)

        @pl.when(s < CH - 1)
        def _():
            for r in (2, 3, 1):
                ocopy(s, r).start()
            ycopy(s, 0).start()
            ob[s, block(i, j), :] = ost[s, :, mycols(j)]

        return carry

    lax.fori_loop(0, CH, chunk, 0)
    olast[...] = ost[CH - 1]
    for h in range(NH):
        first(h).wait_send()
    for s in range(CH):
        if s:
            later(s).wait_send()
        for r in range(1, nm):
            hcopy(s, r).wait_send()
            if s < CH - 1:
                ocopy(s, r).wait_send()
        if s < CH - 1:
            for r in range(nm):
                ycopy(s, r).wait_send()
                yrecv_copy(s, r).wait_recv()


def _attend(x, Wq, Wk, Wv, Kc, Vc, lengths, ne, nm):
    b, d = x.shape
    de, kk = Wq.shape
    dh = Wk.shape[1]
    slots = Kc.shape[1]
    be = b // ne
    bl = be // nm
    rows = bl // CH
    cw = kk // NH
    full = kk * nm
    nh = full // dh
    assert dh == 256 and slots % BK == 0
    bf, f32 = jnp.bfloat16, jnp.float32
    dma = pltpu.SemaphoreType.DMA
    V = pltpu.VMEM
    part = V((CH, nm * rows, kk), f32)
    flat = V((rows * nh, 128), f32)
    stat = V((nh, 128), f32)
    return pl.pallas_call(
        functools.partial(_qa_kernel, ne, nm, dh ** -0.5),
        out_shape=(V((CH - 1, b // CH, kk), bf), V((rows, full), bf), V((b, dh), bf), V((b, dh), bf)),
        in_specs=[_smem()] + [_hbm()] * 6,
        out_specs=(_vmem(),) * 4,
        scratch_shapes=[
            V((2, b, de), bf), V((NH, de, cw), bf), V((2, 2, de, dh), bf), part, part, part,
            V((CH, nm * rows, kk), bf), V((CH, rows, full), bf), flat, flat, flat, flat, V((CH, rows, full), bf),
            V((bl, dh), f32), V((bl, dh), f32), V((RING, slots, dh), bf), V((RING, slots, dh), bf),
            V((nh, slots), f32), V((nh, slots), f32), stat, stat, stat, stat,
            dma((2, 2)), dma((NH,)), dma((2, 2)), dma((NH,)), dma((NH,)), dma((CH,)), dma((CH,)),
            dma((CH, nm)), dma((CH, nm)), dma((CH, nm)), dma((CH, nm)), dma((CH, nm)), dma((CH, nm)),
            dma((RING,)), dma((RING,)),
        ],
        compiler_params=pltpu.CompilerParams(collective_id=0, has_side_effects=True, vmem_limit_bytes=VLIM << 20),
        name="attend",
    )(lengths, x, Wq, Wk, Wv, Kc, Vc)


def _out_kernel(ne, nm, od_ref, o_ref, wo, x, y, wv, xv, ob, pown, psend, precv, ssend, srecv,
                wsem, xsem, osend, orecv, vsend, vrecv, ps, pr, xs_, xr, cs, cr, es, er, fs, fr):
    i = lax.axis_index("emb")
    j = lax.axis_index("model")
    c = lax.rem(j, 2)
    jp = j + 1 - 2 * c
    jx = lax.rem(j + 2, nm)
    ie = 1 - i
    half = wv.shape[2]
    cw = half // SUB
    rows = o_ref.shape[0]
    kk = wv.shape[1]
    dev = ne * nm

    def at(a, b):
        return {"emb": a, "model": b}

    def wcopy(b, u):
        col = pl.multiple_of((1 - c if b == 0 else c) * half + u * cw, cw)
        return pltpu.make_async_copy(wo.at[:, pl.ds(col, cw)], wv.at[b, :, pl.ds(u * cw, cw)], wsem.at[b, u])

    for b in range(2):
        for u in range(SUB):
            wcopy(b, u).start()
    mycol = pl.multiple_of((i * 2 + c) * half, half)
    excol = pl.multiple_of((ie * 2 + c) * half, half)
    xcopy = pltpu.make_async_copy(x.at[:, :, pl.ds(mycol, half)], xv, xsem)
    xcopy.start()

    barrier = pltpu.get_barrier_semaphore()
    pl.semaphore_signal(barrier, inc=1, device_id=at(ie, j), device_id_type=MESH)
    for r in range(1, nm):
        pl.semaphore_signal(barrier, inc=1, device_id=at(i, lax.rem(j + r, nm)), device_id_type=MESH)
    pl.semaphore_wait(barrier, nm)

    def block(a, d):
        return pl.ds(pl.multiple_of((a * nm + d) * rows, rows), rows)

    def heads(d):
        return pl.ds(pl.multiple_of(d * kk, kk), kk)

    def ocopy(r):
        d = lax.rem(j + r, nm)
        return pltpu.make_async_remote_copy(
            src_ref=o_ref.at[:, heads(d)], dst_ref=ob.at[block(i, j), :],
            send_sem=osend.at[r], recv_sem=orecv.at[nm - r], device_id=at(i, d), device_id_type=MESH)

    def orecv_copy(r):
        d = lax.rem(j + r, nm)
        return pltpu.make_async_remote_copy(
            src_ref=ob.at[block(i, d), :], dst_ref=ob.at[block(i, d), :],
            send_sem=osend.at[r], recv_sem=orecv.at[r], device_id=at(i, d), device_id_type=MESH)

    def vcopy(r):
        dst = ob.at[block(i, lax.rem(j + r, nm)), :]
        return pltpu.make_async_remote_copy(
            src_ref=o_ref.at[:, heads(j)] if r == 0 else dst, dst_ref=dst,
            send_sem=vsend.at[r], recv_sem=vrecv.at[r], device_id=at(ie, j), device_id_type=MESH)

    def vrecv_copy(r):
        blk = ob.at[block(ie, lax.rem(j + r, nm)), :]
        return pltpu.make_async_remote_copy(
            src_ref=blk, dst_ref=blk, send_sem=vsend.at[r], recv_sem=vrecv.at[r],
            device_id=at(ie, j), device_id_type=MESH)

    for r in (2, 3, 1):
        ocopy(r).start()
    vcopy(0).start()
    ob[block(i, j), :] = o_ref[:, heads(j)]

    def pcopy(s, u):
        return pltpu.make_async_remote_copy(
            src_ref=psend.at[s, u], dst_ref=precv.at[s, u], send_sem=ps.at[s, u], recv_sem=pr.at[s, u],
            device_id=at(i, jp), device_id_type=MESH)

    def scopy(s, u):
        return pltpu.make_async_remote_copy(
            src_ref=ssend.at[s, u], dst_ref=srecv.at[s, u], send_sem=xs_.at[s, u], recv_sem=xr.at[s, u],
            device_id=at(i, jx), device_id_type=MESH)

    def piece(s, u, base):
        return y.at[:, pl.ds(pl.multiple_of(s * rows, rows), rows), pl.ds(pl.multiple_of(base + u * cw, cw), cw)]

    def ccopy(s, u):
        return pltpu.make_async_remote_copy(
            src_ref=piece(s, u, mycol), dst_ref=piece(s, u, mycol), send_sem=cs.at[s, u], recv_sem=cr.at[s, u],
            device_id=at(i, jp), device_id_type=MESH)

    def ecopy(s, u):
        return pltpu.make_async_remote_copy(
            src_ref=piece(s, u, mycol), dst_ref=piece(s, u, mycol), send_sem=es.at[s, u], recv_sem=er.at[s, u],
            device_id=at(ie, j), device_id_type=MESH)

    def fcopy(s, u):
        return pltpu.make_async_remote_copy(
            src_ref=piece(s, u, excol), dst_ref=piece(s, u, excol), send_sem=fs.at[s, u], recv_sem=fr.at[s, u],
            device_id=at(i, jp), device_id_type=MESH)

    def compute(s, lhs):
        for u in range(SUB):
            @pl.when(s == 0)
            def _():
                wcopy(0, u).wait()

            psend[s, u] = jnp.dot(lhs(), wv[0, :, u * cw:(u + 1) * cw],
                                  preferred_element_type=jnp.float32).astype(jnp.bfloat16)
            pcopy(s, u).start()
        for u in range(SUB):
            @pl.when(s == 0)
            def _():
                wcopy(1, u).wait()

            pown[u] = jnp.dot(lhs(), wv[1, :, u * cw:(u + 1) * cw], preferred_element_type=jnp.float32)
            pcopy(s, u).wait_recv()
            ssend[s, u] = (pown[u] + precv[s, u].astype(jnp.float32)).astype(jnp.bfloat16)
            scopy(s, u).start()

    def finish(s):
        at_rows = pl.ds(pl.multiple_of(s * rows, rows), rows)
        for u in range(SUB):
            scopy(s, u).wait_recv()
            tot = ssend[s, u].astype(jnp.float32) + srecv[s, u].astype(jnp.float32)
            xs = xv[:, at_rows, u * cw:(u + 1) * cw].astype(jnp.float32)
            y[:, at_rows, pl.ds(pl.multiple_of(mycol + u * cw, cw), cw)] = (
                xs + tot.reshape(dev, rows, cw)).astype(jnp.bfloat16)
            ecopy(s, u).start()
            ccopy(s, u).start()

    def forward(s):
        for u in range(SUB):
            ecopy(s, u).wait_recv()
            fcopy(s, u).start()

    def step(s, carry):
        compute(s, lambda: od_ref[s])

        @pl.when(s == 0)
        def _():
            for r in range(1, nm):
                orecv_copy(r).wait_recv()
                vcopy(r).start()
            xcopy.wait()

        @pl.when(s >= 1)
        def _():
            finish(s - 1)

        @pl.when(s >= 2)
        def _():
            forward(s - 2)

        return carry

    lax.fori_loop(0, CH - 1, step, 0)
    for r in range(nm):
        vrecv_copy(r).wait_recv()
    compute(CH - 1, lambda: ob[...])
    finish(CH - 2)
    forward(CH - 3)
    finish(CH - 1)
    forward(CH - 2)
    forward(CH - 1)
    for r in range(1, nm):
        ocopy(r).wait_send()
    for r in range(nm):
        vcopy(r).wait_send()
    for s in range(CH):
        for u in range(SUB):
            pcopy(s, u).wait_send()
            scopy(s, u).wait_send()
            ecopy(s, u).wait_send()
            ccopy(s, u).wait()
            fcopy(s, u).wait()


def _project_out(done, last, Wo, x, ne, nm):
    bl = CH * last.shape[0]
    kk, ncol = Wo.shape
    half = ncol // 2
    dev = ne * nm
    rows = bl // CH
    cw = half // SUB
    b, d = x.shape
    bf, f32 = jnp.bfloat16, jnp.float32
    dma = pltpu.SemaphoreType.DMA
    pieces = pltpu.VMEM((CH, SUB, dev * rows, cw), bf)
    y = pl.pallas_call(
        functools.partial(_out_kernel, ne, nm),
        out_shape=pltpu.VMEM((dev, bl, d), bf),
        in_specs=[_vmem(), _vmem(), _hbm(), _hbm()],
        out_specs=_vmem(),
        scratch_shapes=[
            pltpu.VMEM((2, kk, half), bf), pltpu.VMEM((dev, bl, half), bf), pltpu.VMEM((dev * rows, kk), bf),
            pltpu.VMEM((SUB, dev * rows, cw), f32), pieces, pieces, pieces, pieces,
            dma((2, SUB)), dma,
        ] + [dma((nm,))] * 4 + [dma((CH, SUB))] * 10,
        compiler_params=pltpu.CompilerParams(collective_id=1, has_side_effects=True, vmem_limit_bytes=36 << 20),
        name="project_out",
    )(done, last, Wo, x.reshape(dev, bl, d))
    return y.reshape(b, d)


def solution(mesh):
    ne = mesh.shape['emb']
    nm = mesh.shape['model']

    def local(x, Wq, Wk, Wv, Wo, Kc, Vc, lengths):
        done, last, k_new, v_new = _attend(x, Wq, Wk, Wv, Kc, Vc, lengths, ne, nm)
        y = _project_out(done, last, Wo, x, ne, nm)
        return y, k_new, v_new

    in_specs = (P('rep', None), P('emb', 'model'), P(), P(), P('model', 'emb'),
                P('rep', None, None), P('rep', None, None), P('rep'))
    out_specs = (P('rep', None), P('rep', None), P('rep', None))
    return jax.shard_map(local, mesh=mesh, in_specs=in_specs, out_specs=out_specs, check_vma=False)
```

time: 437 us -> 149 us (0.34)
  waiting for transfers between devices: 265 us -> 0 us
  Pallas kernels: 0 us -> 140 us
  matrix products: 105 us -> 0 us
  other arithmetic: 17.2 us -> 0 us
  blocking collectives: 16.9 us -> 0 us
  between operations: 13.9 us -> 0.65 us
  local copies, waits for them, and re-layouts: 14.3 us -> 8.19 us
    pallas_call x0 -> x2, Pallas kernels: none -> 140 us  [the longest x1 79.5 us: _attend(): pl.pallas_call(functools.partial(_qa_kernel, ne, nm, dh ** (-0.5)), out_s...]
    all_gather x2 -> x0, waiting for transfers between devices: 132 us -> none  [the longest x1 103 us: local(): y = lax.all_gather(yi, 'emb', axis=1, tiled=True)]
    dot_general x7 -> x0, matrix products: 105 us -> none  [the longest x1 33.8 us: _attend(): jnp.einsum('bhd,btd->bht', q, K, preferred_element_type=jnp.float32) * scale]
    psum x1 -> x0, waiting for transfers between devices: 79.9 us -> none  [local(): ys = lax.psum(yp, 'model')]
    reduce_scatter x1 -> x0, waiting for transfers between devices: 47.6 us -> none  [local(): q = lax.psum_scatter(qp, 'emb', scatter_dimension=0, tiled=True)]
    all_to_all x1 -> x0, blocking collectives: 16.9 us -> none  [local(): o = lax.all_to_all(o, 'model', 1, 0, tiled=True)]
    convert_element_type x4 -> x0, other arithmetic: 9.01 us -> none  [the longest x1 7.25 us: local(): yi = (xi.astype(jnp.float32) + ys.astype(jnp.float32)).astype(jnp.bfloat16)]
    reduce_sum x1 -> x0, other arithmetic: 8.09 us -> none  [_attend(): l = jnp.sum(p, axis=-1) + pn]
  transfers between devices with their start and end apart: 5 -> 0, of which waited for: 5 -> 0; matrix products, arithmetic and copies ran while one was open for 3% -> 0% of each run, Pallas kernels for 0% -> 0%
where the time goes in v3:
time: 149 us
  Pallas kernels  140 us (94%)
  local copies, waits for them, and re-layouts  8.19 us (5%)
    pallas_call x1, Pallas kernels, _attend(): pl.pallas_call(functools.partial(_qa_kernel, ne, nm, dh ** (-0.5)), out_s...  79.5 us
    pallas_call x1, Pallas kernels, _project_out(): pl.pallas_call(functools.partial(_out_kernel, ne, nm), out_shape=pltpu.VM...  61 us
    unnamed x5, local copies, waits for them, and re-layouts  8.19 us

profile of v3, /device:TPU:0, one launch (start us, length us, event | category | flops | bytes accessed | tf_op | source)
XLA Modules:
  0.0 149.3 jit_solution(14715124621234087790)
XLA Ops:
  0.6 79.5 %attend.1 = (bf16[3,128,2048]{2,1,0:T(8,128)(2,1)S(1)}, bf16[16,8192]{1,0:T(8,128)(2,1)S(1)}, bf16[512,256]{1,0:T(8,128)(2,1)S(1)}, bf16[512,256]{1,0:T(8,128)(2,1)S(1)}) custom-call(s32[512]{0:T(512)} %lens.1, bf16[512,8192]{1,0:T(8,128)(2,1)} %x.1, bf16[4096,2048]{1,0:T(8,128)(2,1)} %wq.1, bf16[8192,256]{1,0:T(8,128)(2,1)} %wk.1, bf16[8192,256]{1,0:T(8,128)(2,1)} %wv.1, ...), custom_call_target="tpu_custom_call" | custom-call | tf_op jit(solution)/shard_map/attend/pallas_call | solution.py:339
  80.1 0.7 copy.15
  80.8 0.7 copy.16
  81.5 0.0 copy-start
  81.5 3.4 %copy-done = bf16[512,8192]{1,0:T(8,128)(2,1)S(1)} copy-done((bf16[512,8192]{1,0:T(8,128)(2,1)S(1)}, bf16[512,8192]{1,0:T(8,128)(2,1)}, u32[]{:S(2)}) %copy-start) | copy-done | bytes 8388632
  84.9 61.0 %project_out.1 = bf16[8,64,8192]{2,1,0:T(8,128)(2,1)S(1)} custom-call(bf16[3,128,2048]{2,1,0:T(8,128)(2,1)S(1)} %get-tuple-element.7.od_ref, bf16[16,8192]{1,0:T(8,128)(2,1)S(1)} %get-tuple-element.8.o_ref, bf16[2048,4096]{1,0:T(8,128)(2,1)} %wo.1, bf16[8,64,8192]{2,1,0:T(8,128)(2,1)S(1)} %bitcast.3), custom_call_target="tpu_custom_call" | custom-call | tf_op jit(solution)/shard_map/project_out/pallas_call | solution.py:544
  145.9 3.4 %copy.14 = bf16[512,8192]{1,0:T(8,128)(2,1)} copy(bf16[512,8192]{1,0:T(8,128)(2,1)S(1)} %bitcast.2) | data formatting | bytes 16777216
Async XLA Ops:
  81.5 3.4 %copy-start = (bf16[512,8192]{1,0:T(8,128)(2,1)S(1)}, bf16[512,8192]{1,0:T(8,128)(2,1)}, u32[]{:S(2)}) copy-start(bf16[512,8192]{1,0:T(8,128)(2,1)} %x.1) | copy-start | bytes 25165828

commit v4 on v3

--- a/solution.py
+++ b/solution.py
@@ -9,10 +9,11 @@
 
 MESH = pl.DeviceIdType.MESH
 BK = 512
-HOOK = 3
 VLIM = 60
+DEAL = 1
+RELAY = 2
 RING = 6
-CH = 4
+CH = 8
 SUB = 4
 NH = 8
 
@@ -158,6 +159,21 @@
     xcopy(1, 0).wait()
     for h in range(NH):
         spread(qown, h, jnp.dot(xv[0, be:, :], wqv[h], preferred_element_type=jnp.float32))
+    def deal(s):
+        qc[s] = (qown[s] + qrecv[s]).astype(jnp.bfloat16)
+        for r in (2, 3, 1):
+            hcopy(s, r).start()
+        qin[s, :, mycols(j)] = qc[s, pl.ds(pl.multiple_of(j * rows, rows), rows), :]
+
+    def relay(s):
+        for r in range(1, nm):
+            orecv_copy(s, r).wait_recv()
+            ycopy(s, r).start()
+
+    for h in range(NH):
+        first(h).wait_recv()
+    deal(0)
+
     xcopy(0, 1).wait()
     xcopy(1, 1).wait()
     for n in range(2):
@@ -170,23 +186,8 @@
             out[pl.ds(pl.multiple_of((ie if a == 0 else i) * be, be), be), :] = acc.astype(jnp.bfloat16)
         rowf[...] = out[pl.ds(pl.multiple_of(start, bl), bl), :].astype(jnp.float32)
 
-    def deal(s):
-        qc[s] = (qown[s] + qrecv[s]).astype(jnp.bfloat16)
-        for r in (2, 3, 1):
-            hcopy(s, r).start()
-        qin[s, :, mycols(j)] = qc[s, pl.ds(pl.multiple_of(j * rows, rows), rows), :]
-
-    def relay(s):
-        for r in range(1, nm):
-            orecv_copy(s, r).wait_recv()
-            ycopy(s, r).start()
-
-    for h in range(NH):
-        first(h).wait_recv()
-    deal(0)
-
-    def scores(s, n, sref, mref, nref):
-        t = n - s * rows
+    def scores(n, sref, mref, nref):
+        t = n % rows
         seq = pl.ds(pl.multiple_of(t * nh, nh), nh)
         qf = jnp.concatenate([qa[seq, :], qb[seq, :]], 1)
         q = qf.astype(jnp.bfloat16)
@@ -204,8 +205,8 @@
         mref[...] = jnp.broadcast_to(m, mref.shape)
         nref[...] = jnp.broadcast_to(new, nref.shape)
 
-    def values(s, n, sref, mref, nref):
-        t = n - s * rows
+    def values(n, sref, mref, nref):
+        t = n % rows
         seq = pl.ds(pl.multiple_of(t * nh, nh), nh)
         slot = lax.rem(n, RING)
         m = mref[...]
@@ -244,64 +245,75 @@
         def _():
             vcopy(n + RING - 1).start()
 
-    def chunk(s, carry):
-        n0 = s * rows
+    per = rows // 2
+
+    def load_q(s):
         for r in range(1, nm):
             hrecv(s, r).wait_recv()
         for h in range(nh):
             qa[pl.ds(h, rows, stride=nh), :] = qin[s, :, h * dh:h * dh + 128].astype(jnp.float32)
             qb[pl.ds(h, rows, stride=nh), :] = qin[s, :, h * dh + 128:(h + 1) * dh].astype(jnp.float32)
-        kcopy(n0).wait()
-        scores(s, n0, *A)
-
-        def pair(t, c):
-            n = n0 + 2 * t
-
-            @pl.when(t == HOOK)
+
+    def store_o(s):
+        for h in range(nh):
+            ost[s, :, h * dh:h * dh + 128] = oa[pl.ds(h, rows, stride=nh), :].astype(jnp.bfloat16)
+            ost[s, :, h * dh + 128:(h + 1) * dh] = obh[pl.ds(h, rows, stride=nh), :].astype(jnp.bfloat16)
+
+    load_q(0)
+    kcopy(0).wait()
+    scores(0, *A)
+
+    def pair(p, c):
+        n = 2 * p
+        s = p // per
+        t = p % per
+
+        @pl.when(t == DEAL)
+        def _():
+            @pl.when(s + 1 < CH)
             def _():
-                @pl.when(s + 1 < CH)
-                def _():
-                    later(s + 1).wait_recv()
-                    deal(s + 1)
-
-                @pl.when(s >= 1)
-                def _():
-                    relay(s - 1)
-
-            fetch(n)
-            kcopy(n + 1).wait()
-            vcopy(n).wait()
-            values(s, n, *A)
-            scores(s, n + 1, *B)
-            kcopy(n + 2).wait()
-            vcopy(n + 1).wait()
-            values(s, n + 1, *B)
-            scores(s, n + 2, *A)
-            return c
-
-        lax.fori_loop(0, rows // 2 - 1, pair, 0)
-        n = n0 + rows - 2
+                later(s + 1).wait_recv()
+                deal(s + 1)
+
+        @pl.when(t == RELAY)
+        def _():
+            @pl.when(s >= 1)
+            def _():
+                relay(s - 1)
+
         fetch(n)
         kcopy(n + 1).wait()
         vcopy(n).wait()
-        values(s, n, *A)
-        scores(s, n + 1, *B)
+        values(n, *A)
+        scores(n + 1, *B)
+
+        @pl.when(t == per - 1)
+        def _():
+            load_q(s + 1)
+
+        kcopy(n + 2).wait()
         vcopy(n + 1).wait()
-        values(s, n + 1, *B)
-        for h in range(nh):
-            ost[s, :, h * dh:h * dh + 128] = oa[pl.ds(h, rows, stride=nh), :].astype(jnp.bfloat16)
-            ost[s, :, h * dh + 128:(h + 1) * dh] = obh[pl.ds(h, rows, stride=nh), :].astype(jnp.bfloat16)
-
-        @pl.when(s < CH - 1)
-        def _():
+        values(n + 1, *B)
+        scores(n + 2, *A)
+
+        @pl.when(t == per - 1)
+        def _():
+            store_o(s)
             for r in (2, 3, 1):
                 ocopy(s, r).start()
             ycopy(s, 0).start()
             ob[s, block(i, j), :] = ost[s, :, mycols(j)]
 
-        return carry
-
-    lax.fori_loop(0, CH, chunk, 0)
+        return c
+
+    lax.fori_loop(0, bl // 2 - 1, pair, 0)
+    kcopy(bl - 1).wait()
+    vcopy(bl - 2).wait()
+    values(bl - 2, *A)
+    scores(bl - 1, *B)
+    vcopy(bl - 1).wait()
+    values(bl - 1, *B)
+    store_o(CH - 1)
     olast[...] = ost[CH - 1]
     for h in range(NH):
         first(h).wait_send()
@@ -551,10 +563,30 @@
             pltpu.VMEM((SUB, dev * rows, cw), f32), pieces, pieces, pieces, pieces,
             dma((2, SUB)), dma,
         ] + [dma((nm,))] * 4 + [dma((CH, SUB))] * 10,
-        compiler_params=pltpu.CompilerParams(collective_id=1, has_side_effects=True, vmem_limit_bytes=36 << 20),
+        compiler_params=pltpu.CompilerParams(collective_id=1, has_side_effects=True, vmem_limit_bytes=48 << 20),
         name="project_out",
-    )(done, last, Wo, x.reshape(dev, bl, d))
+    )(*[pltpu.with_memory_space_constraint(a, pltpu.VMEM) for a in (done, last)], Wo, x.reshape(dev, bl, d))
     return y.reshape(b, d)
+
+
+def _write_kernel(y, k, v, yo, ko, vo, sem):
+    copies = [pltpu.make_async_copy(a, b, sem.at[n]) for n, (a, b) in enumerate(((y, yo), (k, ko), (v, vo)))]
+    for c in copies:
+        c.start()
+    for c in copies:
+        c.wait()
+
+
+def _write(y, k, v):
+    return pl.pallas_call(
+        _write_kernel,
+        out_shape=tuple(jax.ShapeDtypeStruct(a.shape, a.dtype) for a in (y, k, v)),
+        in_specs=[_vmem()] * 3,
+        out_specs=(_hbm(),) * 3,
+        scratch_shapes=[pltpu.SemaphoreType.DMA((3,))],
+        compiler_params=pltpu.CompilerParams(vmem_limit_bytes=16 << 20),
+        name="write",
+    )(y, k, v)
 
 
 def solution(mesh):
@@ -564,7 +596,7 @@
     def local(x, Wq, Wk, Wv, Wo, Kc, Vc, lengths):
         done, last, k_new, v_new = _attend(x, Wq, Wk, Wv, Kc, Vc, lengths, ne, nm)
         y = _project_out(done, last, Wo, x, ne, nm)
-        return y, k_new, v_new
+        return _write(y, k_new, v_new)
 
     in_specs = (P('rep', None), P('emb', 'model'), P(), P(), P('model', 'emb'),
                 P('rep', None, None), P('rep', None, None), P('rep'))

time: 149 us -> 148 us (level)
  local copies, waits for them, and re-layouts: 8.19 us -> 0 us
  Pallas kernels: 140 us -> 147 us
    unnamed x5 -> x0, local copies, waits for them, and re-layouts: 8.19 us -> none
    pallas_call x0 -> x1, Pallas kernels: none -> 3.57 us  [_write(): pl.pallas_call(_write_kernel, out_shape=tuple((jax.ShapeDtypeStruct(a.sha...]
    pallas_call x1, Pallas kernels: 79.5 us -> 81.6 us  [_attend(): pl.pallas_call(functools.partial(_qa_kernel, ne, nm, dh ** (-0.5)), out_s...]
where the time goes in v4:
time: 148 us; the launch traced here: 147 us
  Pallas kernels  147 us (99%)
    pallas_call x1, Pallas kernels, _attend(): pl.pallas_call(functools.partial(_qa_kernel, ne, nm, dh ** (-0.5)), out_s...  81.6 us
    pallas_call x1, Pallas kernels, _project_out(): pl.pallas_call(functools.partial(_out_kernel, ne, nm), out_shape=pltpu.VM...  61.4 us
    pallas_call x1, Pallas kernels, _write(): pl.pallas_call(_write_kernel, out_shape=tuple((jax.ShapeDtypeStruct(a.sha...  3.57 us

profile of v4, /device:TPU:0, one launch (start us, length us, event | category | flops | bytes accessed | tf_op | source)
XLA Modules:
  0.0 147.4 jit_solution(15332164958915024801)
XLA Ops:
  0.6 81.6 %attend.1 = (bf16[7,64,2048]{2,1,0:T(8,128)(2,1)S(1)}, bf16[8,8192]{1,0:T(8,128)(2,1)S(1)}, bf16[512,256]{1,0:T(8,128)(2,1)S(1)}, bf16[512,256]{1,0:T(8,128)(2,1)S(1)}) custom-call(s32[512]{0:T(512)} %lens.1, bf16[512,8192]{1,0:T(8,128)(2,1)} %x.1, bf16[4096,2048]{1,0:T(8,128)(2,1)} %wq.1, bf16[8192,256]{1,0:T(8,128)(2,1)} %wk.1, bf16[8192,256]{1,0:T(8,128)(2,1)} %wv.1, ...), custom_call_target="tpu_custom_call" | custom-call | tf_op jit(solution)/shard_map/attend/pallas_call | solution.py:351
  82.3 61.4 %project_out.1 = bf16[8,64,8192]{2,1,0:T(8,128)(2,1)S(1)} custom-call(bf16[7,64,2048]{2,1,0:T(8,128)(2,1)S(1)} %get-tuple-element.7.od_ref, bf16[8,8192]{1,0:T(8,128)(2,1)S(1)} %get-tuple-element.8.o_ref, bf16[2048,4096]{1,0:T(8,128)(2,1)} %wo.1, bf16[8,64,8192]{2,1,0:T(8,128)(2,1)} %bitcast.3), custom_call_target="tpu_custom_call" | custom-call | tf_op jit(solution)/shard_map/project_out/pallas_call | solution.py:556
  143.7 3.6 %write.1 = (bf16[512,8192]{1,0:T(8,128)(2,1)}, bf16[512,256]{1,0:T(8,128)(2,1)}, bf16[512,256]{1,0:T(8,128)(2,1)}) custom-call(bf16[512,8192]{1,0:T(8,128)(2,1)S(1)} %bitcast.2, bf16[512,256]{1,0:T(8,128)(2,1)S(1)} %get-tuple-element.9.k, bf16[512,256]{1,0:T(8,128)(2,1)S(1)} %get-tuple-element.10.v), custom_call_target="tpu_custom_call" | custom-call | tf_op jit(solution)/shard_map/write/pallas_call | solution.py:581

commit v5 on v4

--- a/solution.py
+++ b/solution.py
@@ -10,10 +10,11 @@
 MESH = pl.DeviceIdType.MESH
 BK = 512
 VLIM = 60
-DEAL = 1
+DEAL = 3
 RELAY = 2
 RING = 6
 CH = 8
+LAG = 2
 SUB = 4
 NH = 8
 
@@ -259,6 +260,8 @@
             ost[s, :, h * dh:h * dh + 128] = oa[pl.ds(h, rows, stride=nh), :].astype(jnp.bfloat16)
             ost[s, :, h * dh + 128:(h + 1) * dh] = obh[pl.ds(h, rows, stride=nh), :].astype(jnp.bfloat16)
 
+    later(1).wait_recv()
+    deal(1)
     load_q(0)
     kcopy(0).wait()
     scores(0, *A)
@@ -270,10 +273,10 @@
 
         @pl.when(t == DEAL)
         def _():
-            @pl.when(s + 1 < CH)
+            @pl.when(s + 2 < CH)
             def _():
-                later(s + 1).wait_recv()
-                deal(s + 1)
+                later(s + 2).wait_recv()
+                deal(s + 2)
 
         @pl.when(t == RELAY)
         def _():
@@ -367,7 +370,7 @@
     )(lengths, x, Wq, Wk, Wv, Kc, Vc)
 
 
-def _out_kernel(ne, nm, od_ref, o_ref, wo, x, y, wv, xv, ob, pown, psend, precv, ssend, srecv,
+def _out_kernel(ne, nm, od_ref, o_ref, wo, x, y, wv, xv, ob, psend, precv, ssend, srecv,
                 wsem, xsem, osend, orecv, vsend, vrecv, ps, pr, xs_, xr, cs, cr, es, er, fs, fr):
     i = lax.axis_index("emb")
     j = lax.axis_index("model")
@@ -388,9 +391,9 @@
         col = pl.multiple_of((1 - c if b == 0 else c) * half + u * cw, cw)
         return pltpu.make_async_copy(wo.at[:, pl.ds(col, cw)], wv.at[b, :, pl.ds(u * cw, cw)], wsem.at[b, u])
 
-    for b in range(2):
-        for u in range(SUB):
-            wcopy(b, u).start()
+    order = [(0, 0)] + [p for u in range(1, SUB) for p in ((0, u), (1, u - 1))] + [(1, SUB - 1)]
+    for b, u in order:
+        wcopy(b, u).start()
     mycol = pl.multiple_of((i * 2 + c) * half, half)
     excol = pl.multiple_of((ie * 2 + c) * half, half)
     xcopy = pltpu.make_async_copy(x.at[:, :, pl.ds(mycol, half)], xv, xsem)
@@ -466,23 +469,19 @@
             device_id=at(i, jp), device_id_type=MESH)
 
     def compute(s, lhs):
-        for u in range(SUB):
+        for b, u in order:
             @pl.when(s == 0)
             def _():
-                wcopy(0, u).wait()
-
-            psend[s, u] = jnp.dot(lhs(), wv[0, :, u * cw:(u + 1) * cw],
-                                  preferred_element_type=jnp.float32).astype(jnp.bfloat16)
-            pcopy(s, u).start()
-        for u in range(SUB):
-            @pl.when(s == 0)
-            def _():
-                wcopy(1, u).wait()
-
-            pown[u] = jnp.dot(lhs(), wv[1, :, u * cw:(u + 1) * cw], preferred_element_type=jnp.float32)
-            pcopy(s, u).wait_recv()
-            ssend[s, u] = (pown[u] + precv[s, u].astype(jnp.float32)).astype(jnp.bfloat16)
-            scopy(s, u).start()
+                wcopy(b, u).wait()
+
+            part = jnp.dot(lhs(), wv[b, :, u * cw:(u + 1) * cw], preferred_element_type=jnp.float32)
+            if b == 0:
+                psend[s, u] = part.astype(jnp.bfloat16)
+                pcopy(s, u).start()
+            else:
+                pcopy(s, u).wait_recv()
+                ssend[s, u] = (part + precv[s, u].astype(jnp.float32)).astype(jnp.bfloat16)
+                scopy(s, u).start()
 
     def finish(s):
         at_rows = pl.ds(pl.multiple_of(s * rows, rows), rows)
@@ -510,13 +509,13 @@
                 vcopy(r).start()
             xcopy.wait()
 
-        @pl.when(s >= 1)
-        def _():
-            finish(s - 1)
-
-        @pl.when(s >= 2)
-        def _():
-            forward(s - 2)
+        @pl.when(s >= LAG)
+        def _():
+            finish(s - LAG)
+
+        @pl.when(s >= 2 * LAG)
+        def _():
+            forward(s - 2 * LAG)
 
         return carry
 
@@ -524,11 +523,11 @@
     for r in range(nm):
         vrecv_copy(r).wait_recv()
     compute(CH - 1, lambda: ob[...])
-    finish(CH - 2)
-    forward(CH - 3)
-    finish(CH - 1)
-    forward(CH - 2)
-    forward(CH - 1)
+    for s in range(CH - 1, CH + LAG):
+        finish(s - LAG)
+        forward(s - 2 * LAG)
+    for s in range(CH - LAG, CH):
+        forward(s)
     for r in range(1, nm):
         ocopy(r).wait_send()
     for r in range(nm):
@@ -560,7 +559,7 @@
         out_specs=_vmem(),
         scratch_shapes=[
             pltpu.VMEM((2, kk, half), bf), pltpu.VMEM((dev, bl, half), bf), pltpu.VMEM((dev * rows, kk), bf),
-            pltpu.VMEM((SUB, dev * rows, cw), f32), pieces, pieces, pieces, pieces,
+            pieces, pieces, pieces, pieces,
             dma((2, SUB)), dma,
         ] + [dma((nm,))] * 4 + [dma((CH, SUB))] * 10,
         compiler_params=pltpu.CompilerParams(collective_id=1, has_side_effects=True, vmem_limit_bytes=48 << 20),

time: 148 us -> 155 us (1.047)
  Pallas kernels: 147 us -> 154 us
    pallas_call x1, Pallas kernels: 61.4 us -> 68.8 us  [_project_out(): pl.pallas_call(functools.partial(_out_kernel, ne, nm), out_shape=pltpu.VM...]
where the time goes in v5:
time: 155 us
  Pallas kernels  154 us (99%)
    pallas_call x1, Pallas kernels, _attend(): pl.pallas_call(functools.partial(_qa_kernel, ne, nm, dh ** (-0.5)), out_s...  81.9 us
    pallas_call x1, Pallas kernels, _project_out(): pl.pallas_call(functools.partial(_out_kernel, ne, nm), out_shape=pltpu.VM...  68.8 us
    pallas_call x1, Pallas kernels, _write(): pl.pallas_call(_write_kernel, out_shape=tuple((jax.ShapeDtypeStruct(a.sha...  3.57 us

profile of v5, /device:TPU:0, one launch (start us, length us, event | category | flops | bytes accessed | tf_op | source)
XLA Modules:
  0.0 155.0 jit_solution(14626018966609215011)
XLA Ops:
  0.6 81.9 %attend.1 = (bf16[7,64,2048]{2,1,0:T(8,128)(2,1)S(1)}, bf16[8,8192]{1,0:T(8,128)(2,1)S(1)}, bf16[512,256]{1,0:T(8,128)(2,1)S(1)}, bf16[512,256]{1,0:T(8,128)(2,1)S(1)}) custom-call(s32[512]{0:T(512)} %lens.1, bf16[512,8192]{1,0:T(8,128)(2,1)} %x.1, bf16[4096,2048]{1,0:T(8,128)(2,1)} %wq.1, bf16[8192,256]{1,0:T(8,128)(2,1)} %wk.1, bf16[8192,256]{1,0:T(8,128)(2,1)} %wv.1, ...), custom_call_target="tpu_custom_call" | custom-call | tf_op jit(solution)/shard_map/attend/pallas_call | solution.py:354
  82.5 68.8 %project_out.1 = bf16[8,64,8192]{2,1,0:T(8,128)(2,1)S(1)} custom-call(bf16[7,64,2048]{2,1,0:T(8,128)(2,1)S(1)} %get-tuple-element.7.od_ref, bf16[8,8192]{1,0:T(8,128)(2,1)S(1)} %get-tuple-element.8.o_ref, bf16[2048,4096]{1,0:T(8,128)(2,1)} %wo.1, bf16[8,64,8192]{2,1,0:T(8,128)(2,1)} %bitcast.3), custom_call_target="tpu_custom_call" | custom-call | tf_op jit(solution)/shard_map/project_out/pallas_call | solution.py:555
  151.3 3.6 %write.1 = (bf16[512,8192]{1,0:T(8,128)(2,1)}, bf16[512,256]{1,0:T(8,128)(2,1)}, bf16[512,256]{1,0:T(8,128)(2,1)}) custom-call(bf16[512,8192]{1,0:T(8,128)(2,1)S(1)} %bitcast.2, bf16[512,256]{1,0:T(8,128)(2,1)S(1)} %get-tuple-element.9.k, bf16[512,256]{1,0:T(8,128)(2,1)S(1)} %get-tuple-element.10.v), custom_call_target="tpu_custom_call" | custom-call | tf_op jit(solution)/shard_map/write/pallas_call | solution.py:580

commit v6 on v4

--- a/solution.py
+++ b/solution.py
@@ -10,10 +10,12 @@
 MESH = pl.DeviceIdType.MESH
 BK = 512
 VLIM = 60
-DEAL = 1
+DEAL = 3
+CUT = 4
 RELAY = 2
 RING = 6
 CH = 8
+LAG = 2
 SUB = 4
 NH = 8
 
@@ -64,13 +66,25 @@
         row = pl.multiple_of((i if r == 0 else ie) * de, de)
         return pltpu.make_async_copy(src.at[pl.ds(row, de), :], wkv.at[n, r], kvsem.at[n, r])
 
+    class Pieces:
+        def __init__(self, src, dst, sem, n):
+            slot, w = lax.rem(n, RING), slots // CUT
+            self.copies = [pltpu.make_async_copy(src.at[start + n, pl.ds(k * w, w)], dst.at[slot, pl.ds(k * w, w)],
+                                                 sem.at[slot, k]) for k in range(CUT)]
+
+        def start(self):
+            for a in self.copies:
+                a.start()
+
+        def wait(self):
+            for a in self.copies:
+                a.wait()
+
     def kcopy(n):
-        slot = lax.rem(n, RING)
-        return pltpu.make_async_copy(kc.at[start + n], kbuf.at[slot], ksem.at[slot])
+        return Pieces(kc, kbuf, ksem, n)
 
     def vcopy(n):
-        slot = lax.rem(n, RING)
-        return pltpu.make_async_copy(vc.at[start + n], vbuf.at[slot], vsem.at[slot])
+        return Pieces(vc, vbuf, vsem, n)
 
     xcopy(0, 0).start()
     for h in range(NH):
@@ -259,6 +273,8 @@
             ost[s, :, h * dh:h * dh + 128] = oa[pl.ds(h, rows, stride=nh), :].astype(jnp.bfloat16)
             ost[s, :, h * dh + 128:(h + 1) * dh] = obh[pl.ds(h, rows, stride=nh), :].astype(jnp.bfloat16)
 
+    later(1).wait_recv()
+    deal(1)
     load_q(0)
     kcopy(0).wait()
     scores(0, *A)
@@ -270,10 +286,10 @@
 
         @pl.when(t == DEAL)
         def _():
-            @pl.when(s + 1 < CH)
+            @pl.when(s + 2 < CH)
             def _():
-                later(s + 1).wait_recv()
-                deal(s + 1)
+                later(s + 2).wait_recv()
+                deal(s + 2)
 
         @pl.when(t == RELAY)
         def _():
@@ -360,7 +376,7 @@
             V((nh, slots), f32), V((nh, slots), f32), stat, stat, stat, stat,
             dma((2, 2)), dma((NH,)), dma((2, 2)), dma((NH,)), dma((NH,)), dma((CH,)), dma((CH,)),
             dma((CH, nm)), dma((CH, nm)), dma((CH, nm)), dma((CH, nm)), dma((CH, nm)), dma((CH, nm)),
-            dma((RING,)), dma((RING,)),
+            dma((RING, CUT)), dma((RING, CUT)),
         ],
         compiler_params=pltpu.CompilerParams(collective_id=0, has_side_effects=True, vmem_limit_bytes=VLIM << 20),
         name="attend",
@@ -510,13 +526,13 @@
                 vcopy(r).start()
             xcopy.wait()
 
-        @pl.when(s >= 1)
-        def _():
-            finish(s - 1)
-
-        @pl.when(s >= 2)
-        def _():
-            forward(s - 2)
+        @pl.when(s >= LAG)
+        def _():
+            finish(s - LAG)
+
+        @pl.when(s >= 2 * LAG)
+        def _():
+            forward(s - 2 * LAG)
 
         return carry
 
@@ -524,11 +540,11 @@
     for r in range(nm):
         vrecv_copy(r).wait_recv()
     compute(CH - 1, lambda: ob[...])
-    finish(CH - 2)
-    forward(CH - 3)
-    finish(CH - 1)
-    forward(CH - 2)
-    forward(CH - 1)
+    for s in range(CH - 1, CH + LAG):
+        finish(s - LAG)
+        forward(s - 2 * LAG)
+    for s in range(CH - LAG, CH):
+        forward(s)
     for r in range(1, nm):
         ocopy(r).wait_send()
     for r in range(nm):

time: 148 us -> 155 us (1.047)
  Pallas kernels: 147 us -> 154 us
    pallas_call x1, Pallas kernels: 61.4 us -> 66.1 us  [_project_out(): pl.pallas_call(functools.partial(_out_kernel, ne, nm), out_shape=pltpu.VM...]
    pallas_call x1, Pallas kernels: 81.6 us -> 84 us  [_attend(): pl.pallas_call(functools.partial(_qa_kernel, ne, nm, dh ** (-0.5)), out_s...]
where the time goes in v6:
time: 155 us; the launch traced here: 154 us
  Pallas kernels  154 us (99%)
    pallas_call x1, Pallas kernels, _attend(): pl.pallas_call(functools.partial(_qa_kernel, ne, nm, dh ** (-0.5)), out_s...  84 us
    pallas_call x1, Pallas kernels, _project_out(): pl.pallas_call(functools.partial(_out_kernel, ne, nm), out_shape=pltpu.VM...  66.1 us
    pallas_call x1, Pallas kernels, _write(): pl.pallas_call(_write_kernel, out_shape=tuple((jax.ShapeDtypeStruct(a.sha...  3.57 us

profile of v6, /device:TPU:0, one launch (start us, length us, event | category | flops | bytes accessed | tf_op | source)
XLA Modules:
  0.0 154.4 jit_solution(9475593774793518344)
XLA Ops:
  0.6 84.0 %attend.1 = (bf16[7,64,2048]{2,1,0:T(8,128)(2,1)S(1)}, bf16[8,8192]{1,0:T(8,128)(2,1)S(1)}, bf16[512,256]{1,0:T(8,128)(2,1)S(1)}, bf16[512,256]{1,0:T(8,128)(2,1)S(1)}) custom-call(s32[512]{0:T(512)} %lens.1, bf16[512,8192]{1,0:T(8,128)(2,1)} %x.1, bf16[4096,2048]{1,0:T(8,128)(2,1)} %wq.1, bf16[8192,256]{1,0:T(8,128)(2,1)} %wk.1, bf16[8192,256]{1,0:T(8,128)(2,1)} %wv.1, ...), custom_call_target="tpu_custom_call" | custom-call | tf_op jit(solution)/shard_map/attend/pallas_call | solution.py:367
  84.6 66.1 %project_out.1 = bf16[8,64,8192]{2,1,0:T(8,128)(2,1)S(1)} custom-call(bf16[7,64,2048]{2,1,0:T(8,128)(2,1)S(1)} %get-tuple-element.7.od_ref, bf16[8,8192]{1,0:T(8,128)(2,1)S(1)} %get-tuple-element.8.o_ref, bf16[2048,4096]{1,0:T(8,128)(2,1)} %wo.1, bf16[8,64,8192]{2,1,0:T(8,128)(2,1)} %bitcast.3), custom_call_target="tpu_custom_call" | custom-call | tf_op jit(solution)/shard_map/project_out/pallas_call | solution.py:572
  150.7 3.6 %write.1 = (bf16[512,8192]{1,0:T(8,128)(2,1)}, bf16[512,256]{1,0:T(8,128)(2,1)}, bf16[512,256]{1,0:T(8,128)(2,1)}) custom-call(bf16[512,8192]{1,0:T(8,128)(2,1)S(1)} %bitcast.2, bf16[512,256]{1,0:T(8,128)(2,1)S(1)} %get-tuple-element.9.k, bf16[512,256]{1,0:T(8,128)(2,1)S(1)} %get-tuple-element.10.v), custom_call_target="tpu_custom_call" | custom-call | tf_op jit(solution)/shard_map/write/pallas_call | solution.py:597

commit v7 on v4

--- a/solution.py
+++ b/solution.py
@@ -10,10 +10,10 @@
 MESH = pl.DeviceIdType.MESH
 BK = 512
 VLIM = 60
-DEAL = 1
-RELAY = 2
+DEAL = 3
+RELAY = 4
 RING = 6
-CH = 8
+CH = 4
 SUB = 4
 NH = 8
 

time: 148 us -> 142 us (0.959)
  Pallas kernels: 147 us -> 141 us
    pallas_call x1, Pallas kernels: 81.6 us -> 77.1 us  [_attend(): pl.pallas_call(functools.partial(_qa_kernel, ne, nm, dh ** (-0.5)), out_s...]
where the time goes in v7:
time: 142 us
  Pallas kernels  141 us (99%)
    pallas_call x1, Pallas kernels, _attend(): pl.pallas_call(functools.partial(_qa_kernel, ne, nm, dh ** (-0.5)), out_s...  77.1 us
    pallas_call x1, Pallas kernels, _project_out(): pl.pallas_call(functools.partial(_out_kernel, ne, nm), out_shape=pltpu.VM...  60.7 us
    pallas_call x1, Pallas kernels, _write(): pl.pallas_call(_write_kernel, out_shape=tuple((jax.ShapeDtypeStruct(a.sha...  3.57 us

profile of v7, /device:TPU:0, one launch (start us, length us, event | category | flops | bytes accessed | tf_op | source)
XLA Modules:
  0.0 142.1 jit_solution(4821649445123291420)
XLA Ops:
  0.6 77.1 %attend.1 = (bf16[3,128,2048]{2,1,0:T(8,128)(2,1)S(1)}, bf16[16,8192]{1,0:T(8,128)(2,1)S(1)}, bf16[512,256]{1,0:T(8,128)(2,1)S(1)}, bf16[512,256]{1,0:T(8,128)(2,1)S(1)}) custom-call(s32[512]{0:T(512)} %lens.1, bf16[512,8192]{1,0:T(8,128)(2,1)} %x.1, bf16[4096,2048]{1,0:T(8,128)(2,1)} %wq.1, bf16[8192,256]{1,0:T(8,128)(2,1)} %wk.1, bf16[8192,256]{1,0:T(8,128)(2,1)} %wv.1, ...), custom_call_target="tpu_custom_call" | custom-call | tf_op jit(solution)/shard_map/attend/pallas_call | solution.py:351
  77.7 60.7 %project_out.1 = bf16[8,64,8192]{2,1,0:T(8,128)(2,1)S(1)} custom-call(bf16[3,128,2048]{2,1,0:T(8,128)(2,1)S(1)} %get-tuple-element.7.od_ref, bf16[16,8192]{1,0:T(8,128)(2,1)S(1)} %get-tuple-element.8.o_ref, bf16[2048,4096]{1,0:T(8,128)(2,1)} %wo.1, bf16[8,64,8192]{2,1,0:T(8,128)(2,1)} %bitcast.3), custom_call_target="tpu_custom_call" | custom-call | tf_op jit(solution)/shard_map/project_out/pallas_call | solution.py:556
  138.4 3.6 %write.1 = (bf16[512,8192]{1,0:T(8,128)(2,1)}, bf16[512,256]{1,0:T(8,128)(2,1)}, bf16[512,256]{1,0:T(8,128)(2,1)}) custom-call(bf16[512,8192]{1,0:T(8,128)(2,1)S(1)} %bitcast.2, bf16[512,256]{1,0:T(8,128)(2,1)S(1)} %get-tuple-element.9.k, bf16[512,256]{1,0:T(8,128)(2,1)S(1)} %get-tuple-element.10.v), custom_call_target="tpu_custom_call" | custom-call | tf_op jit(solution)/shard_map/write/pallas_call | solution.py:581
